TPU v7x, 256 devices: a whole 4x4x8 slice. The times are simulated.
256 devices in a mesh: sec: 2 (over core), grp: 4 (over x), cp: 32 (over z, y).
Axes of the slice: x: 4, y: 4, z: 8, core: 2. Of those that a mesh axis runs over, the one named last changes fastest.
Arguments:
- prompt_states: bfloat16 [8, 6144, 8192], P('grp', 'cp'), may hold values from -6 to 6
- prompt_queries: bfloat16 [8, 6144, 1024], P('grp', 'cp', 'sec'), may hold values from -180 to 180
- decode_states: bfloat16 [3, 128, 8192], P(None, 'grp'), may hold values from -6 to 6
- decode_queries: bfloat16 [3, 128, 1024], P(None, 'grp', 'sec'), may hold values from -180 to 180
- latent_down: bfloat16 [8192, 256], P(None, 'sec'), may hold values from -0.0625 to 0.0625
- key_up: bfloat16 [128, 1024], P(None, 'sec'), may hold values from -0.5 to 0.5
- value_up: bfloat16 [128, 1024], P(None, 'sec'), may hold values from -0.5 to 0.5
- prompt_lengths: int32 [8], P('grp'), may hold values from 1536 to 6144
- block_order: int32 [64], replicated, may hold values from 0 to 63, each once
- page_owner: int32 [4, 32, 24], P('grp'), may hold values from 0 to 31, as said below
- decode_context: int32 [128], P('grp'), may hold values from 768 to 6144
Outputs:
- prefill_out: bfloat16 [8, 6144, 1024], P('grp', 'cp', 'sec')
- decode_out: bfloat16 [3, 128, 1024], P(None, 'grp', 'sec')
- page_cache: bfloat16 [4, 32, 384, 256], P('grp', 'cp')
Inputs may be any that keep to these rules, and one draw needn't show every extreme that they name: block_order names each block of a prompt once. page_owner[g, s, k] is an index along cp; every owner receives exactly 24 pages of its group, and at most 1 from one device.
All inputs are finite; a program needn't handle non-finite values.
Results may differ from a plain program's by a relative error of at most 0.012.
The roundings to bfloat16 on the way count: a program that leaves them out, or rounds other values in their place, can miss the bound.
Values may be sent and summed in bfloat16 or wider, within the bound.
No kernel may reach another device: no remote copies, remote signals or barrier semaphores. Data moves between devices by JAX's collectives and lax.ppermute only.
A program may use at most 128 MiB of HBM per device.

v0:
```python
import functools
import math

import jax
import jax.numpy as jnp
import numpy as np
from jax import lax
from jax.experimental import pallas as pl
from jax.experimental.pallas import tpu as pltpu
from jax.sharding import PartitionSpec as P


HEAD = 128
RANK = 128
HEADS = 4
BLOCK = 96
PAGE = 16
PPG = 2
ROW_GRP = 32
HALF_GRP = ROW_GRP // PPG
STEPS = 3
PAGES_DEV = 24
ZN, YN = 8, 4
CP = ZN * YN
UNITS = 4
QL = HEADS * BLOCK
DH = 64
DL = HEADS * DH
G = 4
GK = G * BLOCK
NEG = -1e30
SCALE2 = math.log2(math.e) / math.sqrt(HEAD)

CHUNK_Z = [[0], [7, 1], [6, 2], [5, 3], [4]]
SLOT_Z = np.zeros((5, 16), np.int32)
SLOT_Y = np.zeros((5, 16), np.int32)
SLOT_A = np.zeros((5, 16), np.int32)
SLOT_ROW = np.zeros((5, 16), np.int32)
SLOT_OK = np.zeros((5, 16), bool)
for _c, _zs in enumerate(CHUNK_Z):
    for _i, _dz in enumerate(_zs):
        for _dy in range(YN):
            for _a in range(2):
                _j = _i * 8 + _dy * 2 + _a
                SLOT_Z[_c, _j], SLOT_Y[_c, _j], SLOT_A[_c, _j] = _dz, _dy, _a
                SLOT_ROW[_c, _j] = _i * 16 + _dy * 4 + _a
                SLOT_OK[_c, _j] = True

M_IDX, M_ORD, M_ALL, M_DEC, M_OWN, M_LEN, M_POS = 0, 16, 34, 36, 37, 39, 41
PG_HAS, PG_K, PG_SLOT = 0, 1, 2


def lookup(table, indices):
    matches = indices[..., None] == jnp.arange(table.shape[0], dtype=jnp.int32)
    return jnp.sum(jnp.where(matches, table, 0), axis=-1)


def scalar_tables(block_order, lengths, contexts, owners, ci, sec):
    z, y = ci // YN, ci % YN
    source = ((z + SLOT_Z) % ZN) * YN + (y + SLOT_Y) % YN
    order = lookup(block_order, 2 * source + SLOT_A)
    order = jnp.where(SLOT_OK, order, 4096 + np.arange(16, dtype=np.int32))
    rank = jnp.sum((order[:, None, :] < order[:, :, None]).astype(jnp.int32), axis=-1)
    place = rank[:, None, :] == np.arange(16, dtype=np.int32)[None, :, None]
    idx = jnp.sum(jnp.where(place, SLOT_ROW[:, None, :], 0), axis=-1)
    ranked = jnp.sum(jnp.where(place, order[:, None, :], 0), axis=-1)
    own = lookup(block_order, 2 * ci + np.arange(2, dtype=np.int32))
    alive = own * BLOCK < jnp.max(lengths)
    strict = jnp.sum((order[:, None, :] < own[None, :, None]) & alive[None, :, None], axis=-1)
    every = jnp.sum((order[:, None, :] <= own[None, :, None]) & alive[None, :, None], axis=-1)
    row_prompt = np.arange(ROW_GRP, dtype=np.int32) // HALF_GRP
    limits = jnp.minimum(contexts, jnp.where(row_prompt == 0, lengths[0], lengths[1]))
    dec = jnp.sum(order * BLOCK < jnp.max(limits), axis=-1, keepdims=True)
    spread = jnp.broadcast_to(
        jnp.concatenate([own, lengths, jnp.stack([z, y, sec])])[None], (5, 7)
    )
    meta = jnp.concatenate(
        [idx, ranked, strict.astype(jnp.int32), every.astype(jnp.int32), dec.astype(jnp.int32), spread],
        axis=1,
    ).astype(jnp.int32)
    mine = owners == ci
    has = jnp.sum(mine.astype(jnp.int32), axis=1)
    page = jnp.sum(jnp.where(mine, np.arange(PAGES_DEV, dtype=np.int32), 0), axis=1)
    before = np.arange(CP)[None, :] < np.arange(CP)[:, None]
    slot = jnp.sum(jnp.where(before, has[None, :], 0), axis=1)
    pages = jnp.stack([has, page, slot]).astype(jnp.int32)
    limit_rows = limits.reshape(PPG, 1, 1, HALF_GRP)
    limit_lanes = jnp.broadcast_to(limit_rows, (PPG, HEADS, STEPS, HALF_GRP)).reshape(PPG, HEADS, 48)
    limit_lanes = jnp.pad(limit_lanes, ((0, 0), (0, 0), (0, DH - 48))).reshape(PPG, 1, DL)
    return meta, pages, limit_lanes


def queries_kernel(q_ref, dq_ref, u_ref, qt_ref, dqt_ref):
    for p in range(PPG):
        for a in range(2):
            rows = []
            for h in range(HEADS):
                cols = slice(h * HEAD, (h + 1) * HEAD)
                rows.append(
                    lax.dot_general(
                        q_ref[p, a * BLOCK : (a + 1) * BLOCK, cols],
                        u_ref[:, cols],
                        (((1,), (1,)), ((), ())),
                        preferred_element_type=jnp.float32,
                    )
                )
            qt_ref[p * 2 + a] = jnp.concatenate(rows, axis=0).T.astype(jnp.bfloat16)
        rows = []
        for h in range(HEADS):
            cols = slice(h * HEAD, (h + 1) * HEAD)
            q = jnp.concatenate(
                [dq_ref[t, p * HALF_GRP : (p + 1) * HALF_GRP, cols] for t in range(STEPS)]
                + [jnp.zeros((HALF_GRP, HEAD), jnp.bfloat16)],
                axis=0,
            )
            rows.append(
                lax.dot_general(
                    q, u_ref[:, cols], (((1,), (1,)), ((), ())), preferred_element_type=jnp.float32
                )
            )
        dqt_ref[p] = jnp.concatenate(rows, axis=0).T.astype(jnp.bfloat16)


def prepare_queries(prompt_queries, decode_queries, key_up):
    return pl.pallas_call(
        queries_kernel,
        out_shape=(
            jax.ShapeDtypeStruct((UNITS, RANK, QL), jnp.bfloat16),
            jax.ShapeDtypeStruct((PPG, RANK, DL), jnp.bfloat16),
        ),
        cost_estimate=pl.CostEstimate(flops=10**9, bytes_accessed=10**6, transcendentals=0),
        name="queries",
    )(prompt_queries, decode_queries, key_up)


def softmax_step(s, keep, v, m_ref, l_ref, acc_ref, at):
    s = jnp.where(keep, s * SCALE2, NEG)
    old = m_ref[at]
    new = jnp.maximum(old, jnp.max(s, axis=0, keepdims=True))
    factor = jnp.exp2(old - new)
    w = jnp.exp2(s - new)
    m_ref[at] = new
    l_ref[at] = l_ref[at] * factor + jnp.sum(w, axis=0, keepdims=True)
    w = w.astype(jnp.bfloat16)

    def weigh():
        part = lax.dot_general(v, w, (((0,), (0,)), ((), ())), preferred_element_type=jnp.float32)
        acc_ref[at] = acc_ref[at] * factor + part

    return weigh


def chunk_kernel(chunk, n_src, sizes, first, last, *refs):
    refs = list(refs)
    meta = refs.pop(0)
    pages = refs.pop(0) if last else None
    mine = [refs.pop(0) for _ in range(n_src)]
    theirs = [refs.pop(0) for _ in range(n_src)]
    qt, dqt, limit = refs.pop(0), refs.pop(0), refs.pop(0)
    if first:
        new_mine, new_theirs = refs.pop(0), refs.pop(0)
    else:
        state_in = [refs.pop(0) for _ in range(6)]
    if last:
        others = [(refs.pop(0), refs.pop(0)) for _ in range(7)]
        vup = refs.pop(0)
        out_ref, dec_ref, cache_ref = refs.pop(0), refs.pop(0), refs.pop(0)
    else:
        state_out = [refs.pop(0) for _ in range(6)]
    kbuf, vbuf, sbuf, dsbuf, offset, sems = [refs.pop(0) for _ in range(6)]
    if last:
        page_sems = refs.pop(0)
        state = state_in
    else:
        state = state_out
    m, l, acc, dm, dl, dacc = state

    sec = meta[chunk, M_POS + 2]
    spans, at = [], 0
    for n in sizes:
        spans.append((at, n))
        at += n

    def copies(k_src, v_src):
        made = []
        for i, (start, n) in enumerate(spans):
            made.append(pltpu.make_async_copy(k_src[i], kbuf.at[pl.ds(start, n)], sems.at[2 * i]))
            made.append(pltpu.make_async_copy(v_src[i], vbuf.at[pl.ds(start, n)], sems.at[2 * i + 1]))
        return made

    @pl.when(sec == 0)
    def _():
        for copy in copies(mine, theirs):
            copy.start()

    @pl.when(sec != 0)
    def _():
        for copy in copies(theirs, mine):
            copy.start()

    if last:
        z, y = meta[chunk, M_POS], meta[chunk, M_POS + 1]
        table = [(0, dy, others[0][0].at[dy], others[0][1].at[dy]) for dy in range(YN)]
        for i, dz in enumerate([7, 1, 6, 2, 5, 3]):
            table += [(dz, dy, others[1 + i][0].at[dy], others[1 + i][1].at[dy]) for dy in range(YN)]
        for i in range(2):
            table += [(4, 2 * i + e, mine[i].at[pl.ds(e * 4, 4)], theirs[i].at[pl.ds(e * 4, 4)]) for e in range(2)]

        def page_copies(n, dz, dy, own_src, far_src):
            s = lax.rem(z + dz, ZN) * YN + lax.rem(y + dy, YN)
            page, slot = pages[PG_K, s], pages[PG_SLOT, s]
            block, row = page // 6, pl.multiple_of(lax.rem(page, 6) * PAGE, PAGE)
            rows = pl.ds(pl.multiple_of(jnp.minimum(slot, PAGES_DEV - 1) * PAGE, PAGE), PAGE)
            own_at, far_at = sec * RANK, (1 - sec) * RANK
            return (
                pages[PG_HAS, s] > 0,
                pltpu.make_async_copy(
                    own_src.at[block, pl.ds(row, PAGE), :],
                    cache_ref.at[rows, pl.ds(pl.multiple_of(own_at, RANK), RANK)],
                    page_sems.at[2 * n],
                ),
                pltpu.make_async_copy(
                    far_src.at[block, pl.ds(row, PAGE), :],
                    cache_ref.at[rows, pl.ds(pl.multiple_of(far_at, RANK), RANK)],
                    page_sems.at[2 * n + 1],
                ),
            )

        for n, entry in enumerate(table):
            has, one, two = page_copies(n, *entry)

            @pl.when(has)
            def _(one=one, two=two):
                one.start()
                two.start()

    if first:
        m[...] = jnp.full(m.shape, NEG, jnp.float32)
        l[...] = jnp.zeros(l.shape, jnp.float32)
        acc[...] = jnp.zeros(acc.shape, jnp.float32)
        is_key = sec == 0
        lane = lax.broadcasted_iota(jnp.int32, (1, DL), 1)
        step_of = lax.rem(lane, DH) // HALF_GRP
        for p in range(PPG):
            scores, values = [], []
            for t in range(STEPS):
                rows = slice(t * ROW_GRP + p * HALF_GRP, t * ROW_GRP + (p + 1) * HALF_GRP)
                a, b = new_mine[rows, :].astype(jnp.float32), new_theirs[rows, :].astype(jnp.float32)
                k, v = jnp.where(is_key, a, b), jnp.where(is_key, b, a)
                k = jnp.concatenate([k] * (DL // HALF_GRP), axis=0).T
                values.append(jnp.concatenate([v] * (DL // HALF_GRP), axis=0).T)
                s = jnp.sum(dqt[p].astype(jnp.float32) * k, axis=0, keepdims=True) * SCALE2
                scores.append(jnp.where(t <= step_of, s, NEG))
            peak = jnp.maximum(jnp.maximum(scores[0], scores[1]), scores[2])
            weights = [jnp.exp2(s - peak) for s in scores]
            dm[p] = peak
            dl[p] = weights[0] + weights[1] + weights[2]
            total = jnp.zeros((RANK, DL), jnp.float32)
            for w, v in zip(weights, values):
                total = total + w.astype(jnp.bfloat16).astype(jnp.float32) * v
            dacc[p] = total
    elif not last:
        for src, dst in zip(state_in, state_out):
            dst[...] = src[...]

    for copy in copies(mine, theirs):
        copy.wait()

    def rows_of(buf, g, p):
        return jnp.concatenate([buf[meta[chunk, M_IDX + g * G + j] + 2 * p] for j in range(G)], axis=0)

    key_row = lax.broadcasted_iota(jnp.int32, (BLOCK, QL), 0)
    query_row = lax.rem(lax.broadcasted_iota(jnp.int32, (BLOCK, QL), 1), BLOCK)
    offset[...] = key_row - query_row
    groups = [(meta[chunk, M_ALL + a] + G - 1) // G for a in range(2)]
    work = groups[0] + groups[1]

    def part_of(w):
        a = jnp.where(w >= groups[0], 1, 0)
        return a, w - a * groups[0]

    def scores(w, p):
        a, g = part_of(w)
        sbuf[p] = jnp.dot(rows_of(kbuf, g, p), qt[2 * p + a], preferred_element_type=jnp.float32)

    @pl.when(work > 0)
    def _():
        for p in range(PPG):
            scores(0, p)

    def step(w, carry):
        a, g = part_of(w)
        own = meta[chunk, M_OWN + a]
        keep = jnp.concatenate(
            [offset[...] <= (own - meta[chunk, M_ORD + g * G + j]) * BLOCK for j in range(G)], axis=0
        )
        after = jnp.minimum(w + 1, work - 1)
        for p in range(PPG):
            weigh = softmax_step(sbuf[p], keep, rows_of(vbuf, g, p), m, l, acc, 2 * p + a)
            scores(after, p)
            weigh()
        return carry

    lax.fori_loop(0, work, step, 0)

    dec_row = lax.broadcasted_iota(jnp.int32, (BLOCK, DL), 0)
    dec_work = (meta[chunk, M_DEC] + G - 1) // G

    def dec_scores(g, p):
        dsbuf[p] = jnp.dot(rows_of(kbuf, g, p), dqt[p], preferred_element_type=jnp.float32)

    @pl.when(dec_work > 0)
    def _():
        for p in range(PPG):
            dec_scores(0, p)

    def dec_step(g, carry):
        after = jnp.minimum(g + 1, dec_work - 1)
        for p in range(PPG):
            keep = jnp.concatenate(
                [dec_row < limit[p] - meta[chunk, M_ORD + g * G + j] * BLOCK for j in range(G)], axis=0
            )
            weigh = softmax_step(dsbuf[p], keep, rows_of(vbuf, g, p), dm, dl, dacc, p)
            dec_scores(after, p)
            weigh()
        return carry

    lax.fori_loop(0, dec_work, dec_step, 0)

    if last:
        row = lax.broadcasted_iota(jnp.int32, (BLOCK, HEAD), 0)
        for p in range(PPG):
            for a in range(2):
                at = p * 2 + a
                o = (acc[at] / l[at]).T.astype(jnp.bfloat16)
                live = row + meta[chunk, M_OWN + a] * BLOCK < meta[chunk, M_LEN + p]
                for h in range(HEADS):
                    cols = slice(h * HEAD, (h + 1) * HEAD)
                    r = jnp.dot(
                        o[h * BLOCK : (h + 1) * BLOCK], vup[:, cols], preferred_element_type=jnp.float32
                    )
                    out_ref[p, a * BLOCK : (a + 1) * BLOCK, cols] = jnp.where(live, r, 0.0).astype(
                        jnp.bfloat16
                    )
            o = (dacc[p] / dl[p]).T.astype(jnp.bfloat16)
            for h in range(HEADS):
                cols = slice(h * HEAD, (h + 1) * HEAD)
                r = jnp.dot(
                    o[h * DH : (h + 1) * DH], vup[:, cols], preferred_element_type=jnp.float32
                ).astype(jnp.bfloat16)
                for t in range(STEPS):
                    dec_ref[t, p * HALF_GRP : (p + 1) * HALF_GRP, cols] = r[t * HALF_GRP : (t + 1) * HALF_GRP]
        for n, entry in enumerate(table):
            has, one, two = page_copies(n, *entry)

            @pl.when(has)
            def _(one=one, two=two):
                one.wait()
                two.wait()


STATE = (
    jax.ShapeDtypeStruct((UNITS, 1, QL), jnp.float32),
    jax.ShapeDtypeStruct((UNITS, 1, QL), jnp.float32),
    jax.ShapeDtypeStruct((UNITS, RANK, QL), jnp.float32),
    jax.ShapeDtypeStruct((PPG, 1, DL), jnp.float32),
    jax.ShapeDtypeStruct((PPG, 1, DL), jnp.float32),
    jax.ShapeDtypeStruct((PPG, RANK, DL), jnp.float32),
)


def attend_chunk(chunk, meta, mine, theirs, qt, dqt, limit, state=None, new=None, ending=None):
    first, last = state is None, ending is not None
    smem, vmem = pl.BlockSpec(memory_space=pltpu.SMEM), pl.BlockSpec(memory_space=pltpu.VMEM)
    anywhere = pl.BlockSpec(memory_space=pl.ANY)
    sizes = [a.size // (BLOCK * RANK) for a in mine]
    flat = [a.reshape(-1, BLOCK, RANK) for a in [*mine, *theirs]]
    args, specs = [meta], [smem]
    if last:
        args, specs = args + [ending["pages"]], specs + [smem]
    args, specs = args + flat, specs + [anywhere] * len(flat)
    args, specs = args + [qt, dqt, limit], specs + [vmem] * 3
    if first:
        args, specs = args + list(new), specs + [vmem] * 2
    else:
        args, specs = args + list(state), specs + [vmem] * 6
    rows = sum(sizes)
    scratch = [
        pltpu.VMEM((rows, BLOCK, RANK), jnp.bfloat16),
        pltpu.VMEM((rows, BLOCK, RANK), jnp.bfloat16),
        pltpu.VMEM((PPG, GK, QL), jnp.float32),
        pltpu.VMEM((PPG, GK, DL), jnp.float32),
        pltpu.VMEM((BLOCK, QL), jnp.int32),
        pltpu.SemaphoreType.DMA((2 * len(mine),)),
    ]
    if last:
        for pair in ending["others"]:
            args, specs = args + list(pair), specs + [anywhere] * 2
        args, specs = args + [ending["value_up"]], specs + [vmem]
        shapes = (
            jax.ShapeDtypeStruct((PPG, 2 * BLOCK, HEADS * HEAD), jnp.bfloat16),
            jax.ShapeDtypeStruct((STEPS, ROW_GRP, HEADS * HEAD), jnp.bfloat16),
            jax.ShapeDtypeStruct((PAGES_DEV * PAGE, 2 * RANK), jnp.bfloat16),
        )
        scratch.append(pltpu.SemaphoreType.DMA((2 * CP,)))
    else:
        shapes = STATE
    work = rows * BLOCK * (2 * QL + DL) * RANK * 4
    return pl.pallas_call(
        functools.partial(chunk_kernel, chunk, len(mine), sizes, first, last),
        out_shape=shapes,
        in_specs=specs,
        out_specs=[vmem] * len(shapes),
        scratch_shapes=scratch,
        cost_estimate=pl.CostEstimate(flops=2 * work, bytes_accessed=4 * 10**6, transcendentals=work // 512),
        compiler_params=pltpu.CompilerParams(vmem_limit_bytes=48 * 2**20),
    )(*args)


def shifted(x, dz, dy):
    pairs = [
        (z * YN + y, ((z + dz) % ZN) * YN + (y + dy) % YN) for z in range(ZN) for y in range(YN)
    ]
    return lax.ppermute(x, "cp", pairs)


def swapped(x):
    return lax.ppermute(x, "sec", [(0, 1), (1, 0)])


def body(
    prompt_states,
    prompt_queries,
    decode_states,
    decode_queries,
    latent_down,
    key_up,
    value_up,
    prompt_lengths,
    block_order,
    page_owner,
    decode_context,
):
    width = prompt_states.shape[-1]
    ci, sec = lax.axis_index("cp"), lax.axis_index("sec")
    own = jnp.dot(
        prompt_states.reshape(PPG * 2 * BLOCK, width), latent_down, preferred_element_type=jnp.float32
    )
    own = own.astype(jnp.bfloat16).reshape(UNITS, BLOCK, RANK)
    new = jnp.dot(
        decode_states.reshape(STEPS * ROW_GRP, width), latent_down, preferred_element_type=jnp.float32
    ).astype(jnp.bfloat16)
    meta, pages, limit = scalar_tables(
        block_order, prompt_lengths, decode_context, page_owner[0], ci, sec
    )
    qt, dqt = prepare_queries(prompt_queries, decode_queries, key_up)

    plane = jnp.stack([own, shifted(own, 0, -1), shifted(own, 0, 2), shifted(own, 0, 1)])
    new_far = swapped(new)
    up, down = shifted(plane, 1, 0), shifted(plane, -1, 0)
    plane_far = swapped(plane)
    state = attend_chunk(0, meta, [plane], [plane_far], qt, dqt, limit, new=(new, new_far))
    others = [(plane, plane_far)]
    for c in range(1, 4):
        if c < 3:
            up_next = shifted(up, 1, 0)
            down_next = shifted(down, -1, 0)
        else:
            up_next = shifted(up[:2], 1, 0)
            down_next = shifted(down[2:], -1, 0)
        up_far, down_far = swapped(up), swapped(down)
        others += [(up, up_far), (down, down_far)]
        state = attend_chunk(c, meta, [up, down], [up_far, down_far], qt, dqt, limit, state=state)
        up, down = up_next, down_next
    ending = dict(pages=pages, others=others, value_up=value_up)
    far = [swapped(up), swapped(down)]
    prefill_out, decode_out, cache = attend_chunk(4, meta, [up, down], far, qt, dqt, limit, state=state, ending=ending)
    return prefill_out, decode_out, cache.reshape(1, 1, PAGES_DEV * PAGE, 2 * RANK)


def solution(mesh):
    placed = (
        P("grp", "cp", None),
        P("grp", "cp", "sec"),
        P(None, "grp", None),
        P(None, "grp", "sec"),
        P(None, "sec"),
        P(None, "sec"),
        P(None, "sec"),
        P("grp"),
        P(),
        P("grp", None, None),
        P("grp"),
    )
    return jax.shard_map(
        body,
        mesh=mesh,
        in_specs=placed,
        out_specs=(P("grp", "cp", "sec"), P(None, "grp", "sec"), P("grp", "cp", None, None)),
        check_vma=False,
    )
```

profile of v0, /device:TPU:129, one launch (start us, length us, event | category | flops | bytes accessed | tf_op | source)
XLA Modules:
  0.0 103.1 jit_solution(1206571858414648174)
XLA Ops:
  0.6 1.6 %copy-done = bf16[8192,128]{1,0:T(8,128)(2,1)S(1)} copy-done((bf16[8192,128]{1,0:T(8,128)(2,1)S(1)}, bf16[8192,128]{1,0:T(8,128)(2,1)}, u32[]{:S(2)}) %copy-start) | copy-done | bytes 2097176
  2.2 4.7 %convolution_convert_fusion = bf16[384,128]{1,0:T(8,128)(2,1)S(1)} fusion(bf16[384,8192]{1,0:T(8,128)(2,1)} %bitcast.53, bf16[8192,128]{1,0:T(8,128)(2,1)S(1)} %copy-done), kind=kOutput, calls=%fused_computation | convolution fusion | flops 805355520 | bytes 8486912 | tf_op jit(solution)/shard_map/dot_general | solution.py:446
  7.0 2.8 %collective-permute-start = (bf16[4,96,128]{2,1,0:T(8,128)(2,1)S(1)}, bf16[4,96,128]{2,1,0:T(8,128)(2,1)S(1)}, u32[]{:S(2)}, u32[]{:S(2)}) collective-permute-start(bf16[4,96,128]{2,1,0:T(8,128)(2,1)S(1)} %bitcast.55), channel_id=1, source_target_pairs={{0,3},{1,0},{2,1},{3,2},{4,7},{5,4},{6,5},{7,6},{8,11},{9,8},{10,9... | collective-permute-start | bytes 294920 | tf_op jit(solution)/shard_map/ppermute | solution.py:424
  11.5 1.6 %collective-permute-start.20 = (bf16[96,128]{1,0:T(8,128)(2,1)S(1)}, bf16[96,128]{1,0:T(8,128)(2,1)S(1)}, u32[]{:S(2)}, u32[]{:S(2)}) collective-permute-start(bf16[96,128]{1,0:T(8,128)(2,1)S(1)} %convolution_convert_fusion.1.refs_6_), channel_id=1, source_target_pairs={{0,128},{128,0},{1,129},{129,1},{2,130},{130,2},{3,131},{131,3},{4... | collective-permute-start | bytes 73736 | tf_op jit(solution)/shard_map/ppermute | solution.py:428
  14.3 1.9 %fusion.14 = (s32[]{:T(128)}, s32[32]{0:T(128)S(1)}) fusion(s32[32]{0:T(128)S(1)} %copy-done.18, pred[32]{0:T(512)(128)(4,1)S(1)} %copy-done.19, s32[]{:T(128)} %bitcast.1, s32[]{:T(128)} %bitcast), kind=kLoop, calls=%fused_computation.45 | loop fusion | flops 95 | bytes 300 | tf_op jit(solution)/shard_map/reduce_max | solution.py:73
  16.5 1.3 %collective-permute-done.2 = bf16[4,96,128]{2,1,0:T(8,128)(2,1)S(1)} collective-permute-done((bf16[4,96,128]{2,1,0:T(8,128)(2,1)S(1)}, bf16[4,96,128]{2,1,0:T(8,128)(2,1)S(1)}, u32[]{:S(2)}, u32[]{:S(2)}) %collective-permute-start.2) | collective-permute-done | bytes 98336 | tf_op jit(solution)/shard_map/ppermute | solution.py:424
  18.6 1.9 %collective-permute-start.7 = (bf16[4,4,96,128]{3,2,1,0:T(8,128)(2,1)S(1)}, bf16[4,4,96,128]{3,2,1,0:T(8,128)(2,1)}, u32[]{:S(2)}, u32[]{:S(2)}) collective-permute-start(bf16[4,4,96,128]{3,2,1,0:T(8,128)(2,1)S(1)} %pad_maximum_fusion.refs_15_), channel_id=1, source_target_pairs={{0,28},{1,29},{2,30},{3,31},{4,0},{5,1},{6,2},{7,3},{8,4},{9,5},{1... | collective-permute-start | bytes 1179656 | tf_op jit(solution)/shard_map/ppermute | solution.py:424
  22.1 6.8 %collective-permute-done.3.refs_17_ = bf16[4,4,96,128]{3,2,1,0:T(8,128)(2,1)} collective-permute-done((bf16[4,4,96,128]{3,2,1,0:T(8,128)(2,1)S(1)}, bf16[4,4,96,128]{3,2,1,0:T(8,128)(2,1)}, u32[]{:S(2)}, u32[]{:S(2)}) %collective-permute-start.3) | collective-permute-done | bytes 393248 | tf_op jit(solution)/shard_map/ppermute | solution.py:424
  28.9 2.7 %collective-permute-start.8 = (bf16[4,4,96,128]{3,2,1,0:T(8,128)(2,1)}, bf16[4,4,96,128]{3,2,1,0:T(8,128)(2,1)}, u32[]{:S(2)}, u32[]{:S(2)}) collective-permute-start(bf16[4,4,96,128]{3,2,1,0:T(8,128)(2,1)} %collective-permute-done.7.refs_19_), channel_id=1, source_target_pairs={{0,28},{1,29},{2,30},{3,31},{4,0},{5,1},{6,2},{7,3},{8,4},{9,5},{1... | collective-permute-start | bytes 1179656 | tf_op jit(solution)/shard_map/ppermute | solution.py:424
  32.4 2.4 %collective-permute-start.19 = (bf16[4,4,96,128]{3,2,1,0:T(8,128)(2,1)S(1)}, bf16[4,4,96,128]{3,2,1,0:T(8,128)(2,1)}, u32[]{:S(2)}, u32[]{:S(2)}) collective-permute-start(bf16[4,4,96,128]{3,2,1,0:T(8,128)(2,1)S(1)} %pad_maximum_fusion.refs_15_), channel_id=1, source_target_pairs={{0,128},{128,0},{1,129},{129,1},{2,130},{130,2},{3,131},{131,3},{4... | collective-permute-start | bytes 1179656 | tf_op jit(solution)/shard_map/ppermute | solution.py:428
  35.5 3.9 %collective-permute-done.4.refs_21_ = bf16[4,4,96,128]{3,2,1,0:T(8,128)(2,1)} collective-permute-done((bf16[4,4,96,128]{3,2,1,0:T(8,128)(2,1)}, bf16[4,4,96,128]{3,2,1,0:T(8,128)(2,1)}, u32[]{:S(2)}, u32[]{:S(2)}) %collective-permute-start.4) | collective-permute-done | bytes 393248 | tf_op jit(solution)/shard_map/ppermute | solution.py:424
  39.3 2.7 %collective-permute-start.9 = (bf16[4,4,96,128]{3,2,1,0:T(8,128)(2,1)}, bf16[4,4,96,128]{3,2,1,0:T(8,128)(2,1)S(1)}, u32[]{:S(2)}, u32[]{:S(2)}) collective-permute-start(bf16[4,4,96,128]{3,2,1,0:T(8,128)(2,1)} %collective-permute-done.8.refs_23_), channel_id=1, source_target_pairs={{0,28},{1,29},{2,30},{3,31},{4,0},{5,1},{6,2},{7,3},{8,4},{9,5},{1... | collective-permute-start | bytes 1179656 | tf_op jit(solution)/shard_map/ppermute | solution.py:424
  42.0 2.5 %queries.1 = (bf16[4,128,384]{2,1,0:T(8,128)(2,1)}, bf16[2,128,256]{2,1,0:T(8,128)(2,1)}) custom-call(bf16[2,192,512]{2,1,0:T(8,128)(2,1)} %q_ref.1, bf16[3,32,512]{2,1,0:T(8,128)(2,1)} %dq_ref.1, bf16[128,512]{1,0:T(8,128)(2,1)} %u_ref.1), custom_call_target="tpu_custom_call" | custom-call | flops 1000000000 | bytes 1000000 | tf_op jit(solution)/shard_map/queries/pallas_call | solution.py:125
  45.2 3.3 %collective-permute-start.15 = (bf16[4,4,96,128]{3,2,1,0:T(8,128)(2,1)}, bf16[4,4,96,128]{3,2,1,0:T(8,128)(2,1)S(1)}, u32[]{:S(2)}, u32[]{:S(2)}) collective-permute-start(bf16[4,4,96,128]{3,2,1,0:T(8,128)(2,1)} %collective-permute-done.4.refs_21_), channel_id=1, source_target_pairs={{0,128},{128,0},{1,129},{129,1},{2,130},{130,2},{3,131},{131,3},{4... | collective-permute-start | bytes 1179656 | tf_op jit(solution)/shard_map/ppermute | solution.py:428
  48.6 1.0 copy-done.3
  49.6 0.9 copy-done.7
  50.5 6.1 %shard_map.229 = (f32[4,1,384]{2,1,0:T(1,128)S(1)}, f32[4,1,384]{2,1,0:T(1,128)S(1)}, f32[4,128,384]{2,1,0:T(8,128)S(1)}, f32[2,1,256]{2,1,0:T(1,128)S(1)}, f32[...) custom-call(s32[5,44]{1,0:T(8,128)S(1)} %concatenate.7.refs_0_, bf16[16,96,128]{2,1,0:T(8,128)(2,1)S(1)} %bitcast.42, ...), custom_call_target="tpu_custom_call" | custom-call | flops 1610612736 | bytes 4000000 | tf_op jit(solution)/shard_map/pallas_call | solution.py:409
  57.4 10.4 %shard_map.230 = (f32[4,1,384]{2,1,0:T(1,128)S(1)}, f32[4,1,384]{2,1,0:T(1,128)S(1)}, f32[4,128,384]{2,1,0:T(8,128)S(1)}, f32[2,1,256]{2,1,0:T(1,128)S(1)}, f32[...) custom-call(s32[5,44]{1,0:T(8,128)S(1)} %concatenate.7.refs_0_, bf16[16,96,128]{2,1,0:T(8,128)(2,1)} %bitcast.28.refs_1_, ...), custom_call_target="tpu_custom_call" | custom-call | flops 3221225472 | bytes 4000000 | tf_op jit(solution)/shard_map/pallas_call | solution.py:409
  68.0 2.7 %collective-permute-start.10 = (bf16[2,4,96,128]{3,2,1,0:T(8,128)(2,1)S(1)}, bf16[2,4,96,128]{3,2,1,0:T(8,128)(2,1)S(1)}, u32[]{:S(2)}, u32[]{:S(2)}) collective-permute-start(bf16[2,4,96,128]{3,2,1,0:T(8,128)(2,1)S(1)} %slice.17), channel_id=1, source_target_pairs={{0,28},{1,29},{2,30},{3,31},{4,0},{5,1},{6,2},{7,3},{8,4},{9,5},{1... | collective-permute-start | bytes 589832 | tf_op jit(solution)/shard_map/ppermute | solution.py:424
  70.7 10.5 %shard_map.231 = (f32[4,1,384]{2,1,0:T(1,128)S(1)}, f32[4,1,384]{2,1,0:T(1,128)S(1)}, f32[4,128,384]{2,1,0:T(8,128)S(1)}, f32[2,1,256]{2,1,0:T(1,128)S(1)}, f32[...) custom-call(s32[5,44]{1,0:T(8,128)S(1)} %concatenate.7.refs_0_, bf16[16,96,128]{2,1,0:T(8,128)(2,1)} %bitcast.24.refs_1_, ...), custom_call_target="tpu_custom_call" | custom-call | flops 3221225472 | bytes 4000000 | tf_op jit(solution)/shard_map/pallas_call | solution.py:409
  81.3 0.8 collective-permute-start.11
  82.3 10.2 %shard_map.232 = (f32[4,1,384]{2,1,0:T(1,128)S(1)}, f32[4,1,384]{2,1,0:T(1,128)S(1)}, f32[4,128,384]{2,1,0:T(8,128)S(1)}, f32[2,1,256]{2,1,0:T(1,128)S(1)}, f32[...) custom-call(s32[5,44]{1,0:T(8,128)S(1)} %concatenate.7.refs_0_, bf16[16,96,128]{2,1,0:T(8,128)(2,1)S(1)} %bitcast.43, ...), custom_call_target="tpu_custom_call" | custom-call | flops 3221225472 | bytes 4000000 | tf_op jit(solution)/shard_map/pallas_call | solution.py:409
  92.5 0.9 copy-done.2
  93.4 9.5 %shard_map.233 = (bf16[2,192,512]{2,1,0:T(8,128)(2,1)}, bf16[3,32,512]{2,1,0:T(8,128)(2,1)}, bf16[384,256]{1,0:T(8,128)(2,1)}) custom-call(s32[5,44]{1,0:T(8,128)S(1)} %concatenate.7.refs_0_, s32[3,32]{1,0:T(4,128)S(1)} %pad_add_fusion.refs_1_, bf16[8,96,128]{2,1,0:T(8,128)(2,1)S(1)} %bitcast.49, bf16[8,96,128]{2,1,0:T(8,128)(2,1)S(1)} %bitcast.50, ...), custom_call_target="tpu_custom_call" | custom-call | flops 1610612736 | bytes 4000000 | tf_op jit(solution)/shard_map/pallas_call | solution.py:409
  (96 shorter events, 8.8 us)
Async XLA Ops:
  7.0 9.4 %collective-permute-start = (bf16[4,96,128]{2,1,0:T(8,128)(2,1)S(1)}, bf16[4,96,128]{2,1,0:T(8,128)(2,1)S(1)}, u32[]{:S(2)}, u32[]{:S(2)}) collective-permute-start(bf16[4,96,128]{2,1,0:T(8,128)(2,1)S(1)} %bitcast.55), channel_id=1, source_target_pairs={{0,3},{1,0},{2,1},{3,2},{4,7},{5,4},{6,5},{7,6},{8,11},{9,8},{10,9... | collective-permute-start | bytes 294920 | tf_op jit(solution)/shard_map/ppermute | solution.py:424
  9.8 6.6 %collective-permute-start.1 = (bf16[4,96,128]{2,1,0:T(8,128)(2,1)S(1)}, bf16[4,96,128]{2,1,0:T(8,128)(2,1)S(1)}, u32[]{:S(2)}, u32[]{:S(2)}) collective-permute-start(bf16[4,96,128]{2,1,0:T(8,128)(2,1)S(1)} %bitcast.56), channel_id=1, source_target_pairs={{0,2},{1,3},{2,0},{3,1},{4,6},{5,7},{6,4},{7,5},{8,10},{9,11},{10,... | collective-permute-start | bytes 294920 | tf_op jit(solution)/shard_map/ppermute | solution.py:424
  10.2 7.5 %collective-permute-start.2 = (bf16[4,96,128]{2,1,0:T(8,128)(2,1)S(1)}, bf16[4,96,128]{2,1,0:T(8,128)(2,1)S(1)}, u32[]{:S(2)}, u32[]{:S(2)}) collective-permute-start(bf16[4,96,128]{2,1,0:T(8,128)(2,1)S(1)} %bitcast.57), channel_id=1, source_target_pairs={{0,1},{1,2},{2,3},{3,0},{4,5},{5,6},{6,7},{7,4},{8,9},{9,10},{10,1... | collective-permute-start | bytes 294920 | tf_op jit(solution)/shard_map/ppermute | solution.py:424
  10.9 24.1 %copy-start.9 = (s32[1,32,24]{1,2,0:T(8,128)S(1)}, s32[1,32,24]{1,2,0:T(8,128)}, u32[]{:S(2)}) copy-start(s32[1,32,24]{1,2,0:T(8,128)} %param.31) | copy-start | bytes 9220
  11.5 23.5 %collective-permute-start.20 = (bf16[96,128]{1,0:T(8,128)(2,1)S(1)}, bf16[96,128]{1,0:T(8,128)(2,1)S(1)}, u32[]{:S(2)}, u32[]{:S(2)}) collective-permute-start(bf16[96,128]{1,0:T(8,128)(2,1)S(1)} %convolution_convert_fusion.1.refs_6_), channel_id=1, source_target_pairs={{0,128},{128,0},{1,129},{129,1},{2,130},{130,2},{3,131},{131,3},{4... | collective-permute-start | bytes 73736 | tf_op jit(solution)/shard_map/ppermute | solution.py:428
  17.8 27.3 %copy-start.15 = (pred[32,32]{1,0:T(32,128)(4,1)S(1)}, pred[32,32]{1,0:T(32,128)(4,1)}, u32[]{:S(2)}) copy-start(pred[32,32]{1,0:T(32,128)(4,1)} %constant.94.clone) | copy-start | bytes 3076
  17.8 11.1 %collective-permute-start.3 = (bf16[4,4,96,128]{3,2,1,0:T(8,128)(2,1)S(1)}, bf16[4,4,96,128]{3,2,1,0:T(8,128)(2,1)}, u32[]{:S(2)}, u32[]{:S(2)}) collective-permute-start(bf16[4,4,96,128]{3,2,1,0:T(8,128)(2,1)S(1)} %pad_maximum_fusion.refs_15_), channel_id=1, source_target_pairs={{0,4},{1,5},{2,6},{3,7},{4,8},{5,9},{6,10},{7,11},{8,12},{9,13},{1... | collective-permute-start | bytes 1179656 | tf_op jit(solution)/shard_map/ppermute | solution.py:424
  18.6 10.3 %collective-permute-start.7 = (bf16[4,4,96,128]{3,2,1,0:T(8,128)(2,1)S(1)}, bf16[4,4,96,128]{3,2,1,0:T(8,128)(2,1)}, u32[]{:S(2)}, u32[]{:S(2)}) collective-permute-start(bf16[4,4,96,128]{3,2,1,0:T(8,128)(2,1)S(1)} %pad_maximum_fusion.refs_15_), channel_id=1, source_target_pairs={{0,28},{1,29},{2,30},{3,31},{4,0},{5,1},{6,2},{7,3},{8,4},{9,5},{1... | collective-permute-start | bytes 1179656 | tf_op jit(solution)/shard_map/ppermute | solution.py:424
  28.9 10.4 %collective-permute-start.4 = (bf16[4,4,96,128]{3,2,1,0:T(8,128)(2,1)}, bf16[4,4,96,128]{3,2,1,0:T(8,128)(2,1)}, u32[]{:S(2)}, u32[]{:S(2)}) collective-permute-start(bf16[4,4,96,128]{3,2,1,0:T(8,128)(2,1)} %collective-permute-done.3.refs_17_), channel_id=1, source_target_pairs={{0,4},{1,5},{2,6},{3,7},{4,8},{5,9},{6,10},{7,11},{8,12},{9,13},{1... | collective-permute-start | bytes 1179656 | tf_op jit(solution)/shard_map/ppermute | solution.py:424
  28.9 10.4 %collective-permute-start.8 = (bf16[4,4,96,128]{3,2,1,0:T(8,128)(2,1)}, bf16[4,4,96,128]{3,2,1,0:T(8,128)(2,1)}, u32[]{:S(2)}, u32[]{:S(2)}) collective-permute-start(bf16[4,4,96,128]{3,2,1,0:T(8,128)(2,1)} %collective-permute-done.7.refs_19_), channel_id=1, source_target_pairs={{0,28},{1,29},{2,30},{3,31},{4,0},{5,1},{6,2},{7,3},{8,4},{9,5},{1... | collective-permute-start | bytes 1179656 | tf_op jit(solution)/shard_map/ppermute | solution.py:424
  32.4 12.8 %collective-permute-start.19 = (bf16[4,4,96,128]{3,2,1,0:T(8,128)(2,1)S(1)}, bf16[4,4,96,128]{3,2,1,0:T(8,128)(2,1)}, u32[]{:S(2)}, u32[]{:S(2)}) collective-permute-start(bf16[4,4,96,128]{3,2,1,0:T(8,128)(2,1)S(1)} %pad_maximum_fusion.refs_15_), channel_id=1, source_target_pairs={{0,128},{128,0},{1,129},{129,1},{2,130},{130,2},{3,131},{131,3},{4... | collective-permute-start | bytes 1179656 | tf_op jit(solution)/shard_map/ppermute | solution.py:428
  34.9 13.7 %collective-permute-start.17 = (bf16[4,4,96,128]{3,2,1,0:T(8,128)(2,1)}, bf16[4,4,96,128]{3,2,1,0:T(8,128)(2,1)}, u32[]{:S(2)}, u32[]{:S(2)}) collective-permute-start(bf16[4,4,96,128]{3,2,1,0:T(8,128)(2,1)} %collective-permute-done.3.refs_17_), channel_id=1, source_target_pairs={{0,128},{128,0},{1,129},{129,1},{2,130},{130,2},{3,131},{131,3},{4... | collective-permute-start | bytes 1179656 | tf_op jit(solution)/shard_map/ppermute | solution.py:428
  35.0 22.4 %collective-permute-start.18 = (bf16[4,4,96,128]{3,2,1,0:T(8,128)(2,1)}, bf16[4,4,96,128]{3,2,1,0:T(8,128)(2,1)}, u32[]{:S(2)}, u32[]{:S(2)}) collective-permute-start(bf16[4,4,96,128]{3,2,1,0:T(8,128)(2,1)} %collective-permute-done.7.refs_19_), channel_id=1, source_target_pairs={{0,128},{128,0},{1,129},{129,1},{2,130},{130,2},{3,131},{131,3},{4... | collective-permute-start | bytes 1179656 | tf_op jit(solution)/shard_map/ppermute | solution.py:428
  39.3 17.3 %collective-permute-start.5 = (bf16[4,4,96,128]{3,2,1,0:T(8,128)(2,1)}, bf16[4,4,96,128]{3,2,1,0:T(8,128)(2,1)S(1)}, u32[]{:S(2)}, u32[]{:S(2)}) collective-permute-start(bf16[4,4,96,128]{3,2,1,0:T(8,128)(2,1)} %collective-permute-done.4.refs_21_), channel_id=1, source_target_pairs={{0,4},{1,5},{2,6},{3,7},{4,8},{5,9},{6,10},{7,11},{8,12},{9,13},{1... | collective-permute-start | bytes 1179656 | tf_op jit(solution)/shard_map/ppermute | solution.py:424
  39.3 17.9 %collective-permute-start.9 = (bf16[4,4,96,128]{3,2,1,0:T(8,128)(2,1)}, bf16[4,4,96,128]{3,2,1,0:T(8,128)(2,1)S(1)}, u32[]{:S(2)}, u32[]{:S(2)}) collective-permute-start(bf16[4,4,96,128]{3,2,1,0:T(8,128)(2,1)} %collective-permute-done.8.refs_23_), channel_id=1, source_target_pairs={{0,28},{1,29},{2,30},{3,31},{4,0},{5,1},{6,2},{7,3},{8,4},{9,5},{1... | collective-permute-start | bytes 1179656 | tf_op jit(solution)/shard_map/ppermute | solution.py:424
  45.2 22.8 %collective-permute-start.15 = (bf16[4,4,96,128]{3,2,1,0:T(8,128)(2,1)}, bf16[4,4,96,128]{3,2,1,0:T(8,128)(2,1)S(1)}, u32[]{:S(2)}, u32[]{:S(2)}) collective-permute-start(bf16[4,4,96,128]{3,2,1,0:T(8,128)(2,1)} %collective-permute-done.4.refs_21_), channel_id=1, source_target_pairs={{0,128},{128,0},{1,129},{129,1},{2,130},{130,2},{3,131},{131,3},{4... | collective-permute-start | bytes 1179656 | tf_op jit(solution)/shard_map/ppermute | solution.py:428
  48.5 22.2 %collective-permute-start.16 = (bf16[4,4,96,128]{3,2,1,0:T(8,128)(2,1)}, bf16[4,4,96,128]{3,2,1,0:T(8,128)(2,1)S(1)}, u32[]{:S(2)}, u32[]{:S(2)}) collective-permute-start(bf16[4,4,96,128]{3,2,1,0:T(8,128)(2,1)} %collective-permute-done.8.refs_23_), channel_id=1, source_target_pairs={{0,128},{128,0},{1,129},{129,1},{2,130},{130,2},{3,131},{131,3},{4... | collective-permute-start | bytes 1179656 | tf_op jit(solution)/shard_map/ppermute | solution.py:428
  56.6 25.6 %collective-permute-start.13 = (bf16[4,4,96,128]{3,2,1,0:T(8,128)(2,1)S(1)}, bf16[4,4,96,128]{3,2,1,0:T(8,128)(2,1)S(1)}, u32[]{:S(2)}, u32[]{:S(2)}) collective-permute-start(bf16[4,4,96,128]{3,2,1,0:T(8,128)(2,1)S(1)} %collective-permute-done.5.refs_25_), channel_id=1, source_target_pairs={{0,128},{128,0},{1,129},{129,1},{2,130},{130,2},{3,131},{131,3},{4... | collective-permute-start | bytes 1179656 | tf_op jit(solution)/shard_map/ppermute | solution.py:428
  57.3 24.9 %copy-start.1 = (bf16[4,4,96,128]{3,2,1,0:T(8,128)(2,1)}, bf16[4,4,96,128]{3,2,1,0:T(8,128)(2,1)S(1)}, u32[]{:S(2)}) copy-start(bf16[4,4,96,128]{3,2,1,0:T(8,128)(2,1)S(1)} %collective-permute-done.9.refs_27_) | copy-start | bytes 1179652
  57.3 24.9 %collective-permute-start.14 = (bf16[4,4,96,128]{3,2,1,0:T(8,128)(2,1)S(1)}, bf16[4,4,96,128]{3,2,1,0:T(8,128)(2,1)S(1)}, u32[]{:S(2)}, u32[]{:S(2)}) collective-permute-start(bf16[4,4,96,128]{3,2,1,0:T(8,128)(2,1)S(1)} %collective-permute-done.9.refs_27_), channel_id=1, source_target_pairs={{0,128},{128,0},{1,129},{129,1},{2,130},{130,2},{3,131},{131,3},{4... | collective-permute-start | bytes 1179656 | tf_op jit(solution)/shard_map/ppermute | solution.py:428
  67.9 13.4 %collective-permute-start.6 = (bf16[2,4,96,128]{3,2,1,0:T(8,128)(2,1)S(1)}, bf16[2,4,96,128]{3,2,1,0:T(8,128)(2,1)S(1)}, u32[]{:S(2)}, u32[]{:S(2)}) collective-permute-start(bf16[2,4,96,128]{3,2,1,0:T(8,128)(2,1)S(1)} %slice.16), channel_id=1, source_target_pairs={{0,4},{1,5},{2,6},{3,7},{4,8},{5,9},{6,10},{7,11},{8,12},{9,13},{1... | collective-permute-start | bytes 589832 | tf_op jit(solution)/shard_map/ppermute | solution.py:424
  68.0 14.1 %collective-permute-start.10 = (bf16[2,4,96,128]{3,2,1,0:T(8,128)(2,1)S(1)}, bf16[2,4,96,128]{3,2,1,0:T(8,128)(2,1)S(1)}, u32[]{:S(2)}, u32[]{:S(2)}) collective-permute-start(bf16[2,4,96,128]{3,2,1,0:T(8,128)(2,1)S(1)} %slice.17), channel_id=1, source_target_pairs={{0,28},{1,29},{2,30},{3,31},{4,0},{5,1},{6,2},{7,3},{8,4},{9,5},{1... | collective-permute-start | bytes 589832 | tf_op jit(solution)/shard_map/ppermute | solution.py:424
  81.3 12.2 %collective-permute-start.11 = (bf16[2,4,96,128]{3,2,1,0:T(8,128)(2,1)S(1)}, bf16[2,4,96,128]{3,2,1,0:T(8,128)(2,1)S(1)}, u32[]{:S(2)}, u32[]{:S(2)}) collective-permute-start(bf16[2,4,96,128]{3,2,1,0:T(8,128)(2,1)S(1)} %collective-permute-done.6), channel_id=1, source_target_pairs={{0,128},{128,0},{1,129},{129,1},{2,130},{130,2},{3,131},{131,3},{4... | collective-permute-start | bytes 589832 | tf_op jit(solution)/shard_map/ppermute | solution.py:428
  82.1 11.3 %collective-permute-start.12 = (bf16[2,4,96,128]{3,2,1,0:T(8,128)(2,1)S(1)}, bf16[2,4,96,128]{3,2,1,0:T(8,128)(2,1)S(1)}, u32[]{:S(2)}, u32[]{:S(2)}) collective-permute-start(bf16[2,4,96,128]{3,2,1,0:T(8,128)(2,1)S(1)} %collective-permute-done.10), channel_id=1, source_target_pairs={{0,128},{128,0},{1,129},{129,1},{2,130},{130,2},{3,131},{131,3},{4... | collective-permute-start | bytes 589832 | tf_op jit(solution)/shard_map/ppermute | solution.py:428
  (18 other events, 144.8 us)
where the time goes:
time: 103 us
  Pallas kernels  49.3 us (48%)
  starting transfers between devices  24.5 us (24%)
  waiting for transfers between devices  12 us (12%)
  local copies, waits for them, and re-layouts  5.62 us (5%)
  matrix products  5.3 us (5%)
  other arithmetic  5.28 us (5%)
  between operations  1.16 us (1%)
    pallas_call x5, Pallas kernels, attend_chunk(): pl.pallas_call(functools.partial(chunk_kernel, chunk, len(mine), sizes, f...  46.7 us
    ppermute x11, starting transfers between devices, shifted(): return lax.ppermute(x, 'cp', pairs)  14.8 us
    ppermute x11, waiting for transfers between devices, shifted(): return lax.ppermute(x, 'cp', pairs)  11.9 us
    ppermute x10, starting transfers between devices, swapped(): return lax.ppermute(x, 'sec', [(0, 1), (1, 0)])  9.75 us
    dot_general x1, matrix products, body(): jnp.dot(prompt_states.reshape(PPG * 2 * BLOCK, width), latent_down, prefe...  4.68 us
    unnamed x42, local copies, waits for them, and re-layouts  4.48 us
    pallas_call x1, Pallas kernels, prepare_queries(): pl.pallas_call(queries_kernel, out_shape=(jax.ShapeDtypeStruct((UNITS, RA...  2.53 us
  transfers between devices with their start and end apart: 21, of which 3 were waited for; matrix products, arithmetic and copies ran while one was open for 7% of the time, Pallas kernels for 39%

commit v1 on v0

--- a/solution.py
+++ b/solution.py
@@ -46,7 +46,6 @@
                 SLOT_ROW[_c, _j] = _i * 16 + _dy * 4 + _a
                 SLOT_OK[_c, _j] = True
 
-M_IDX, M_ORD, M_ALL, M_DEC, M_OWN, M_LEN, M_POS = 0, 16, 34, 36, 37, 39, 41
 PG_HAS, PG_K, PG_SLOT = 0, 1, 2
 
 
@@ -55,42 +54,25 @@
     return jnp.sum(jnp.where(matches, table, 0), axis=-1)
 
 
-def scalar_tables(block_order, lengths, contexts, owners, ci, sec):
-    z, y = ci // YN, ci % YN
-    source = ((z + SLOT_Z) % ZN) * YN + (y + SLOT_Y) % YN
-    order = lookup(block_order, 2 * source + SLOT_A)
-    order = jnp.where(SLOT_OK, order, 4096 + np.arange(16, dtype=np.int32))
-    rank = jnp.sum((order[:, None, :] < order[:, :, None]).astype(jnp.int32), axis=-1)
-    place = rank[:, None, :] == np.arange(16, dtype=np.int32)[None, :, None]
-    idx = jnp.sum(jnp.where(place, SLOT_ROW[:, None, :], 0), axis=-1)
-    ranked = jnp.sum(jnp.where(place, order[:, None, :], 0), axis=-1)
-    own = lookup(block_order, 2 * ci + np.arange(2, dtype=np.int32))
-    alive = own * BLOCK < jnp.max(lengths)
-    strict = jnp.sum((order[:, None, :] < own[None, :, None]) & alive[None, :, None], axis=-1)
-    every = jnp.sum((order[:, None, :] <= own[None, :, None]) & alive[None, :, None], axis=-1)
-    row_prompt = np.arange(ROW_GRP, dtype=np.int32) // HALF_GRP
-    limits = jnp.minimum(contexts, jnp.where(row_prompt == 0, lengths[0], lengths[1]))
-    dec = jnp.sum(order * BLOCK < jnp.max(limits), axis=-1, keepdims=True)
-    spread = jnp.broadcast_to(
-        jnp.concatenate([own, lengths, jnp.stack([z, y, sec])])[None], (5, 7)
-    )
-    meta = jnp.concatenate(
-        [idx, ranked, strict.astype(jnp.int32), every.astype(jnp.int32), dec.astype(jnp.int32), spread],
-        axis=1,
-    ).astype(jnp.int32)
+def page_table(owners, ci):
     mine = owners == ci
     has = jnp.sum(mine.astype(jnp.int32), axis=1)
     page = jnp.sum(jnp.where(mine, np.arange(PAGES_DEV, dtype=np.int32), 0), axis=1)
     before = np.arange(CP)[None, :] < np.arange(CP)[:, None]
     slot = jnp.sum(jnp.where(before, has[None, :], 0), axis=1)
-    pages = jnp.stack([has, page, slot]).astype(jnp.int32)
-    limit_rows = limits.reshape(PPG, 1, 1, HALF_GRP)
-    limit_lanes = jnp.broadcast_to(limit_rows, (PPG, HEADS, STEPS, HALF_GRP)).reshape(PPG, HEADS, 48)
-    limit_lanes = jnp.pad(limit_lanes, ((0, 0), (0, 0), (0, DH - 48))).reshape(PPG, 1, DL)
-    return meta, pages, limit_lanes
-
-
-def queries_kernel(q_ref, dq_ref, u_ref, qt_ref, dqt_ref):
+    return jnp.stack([has, page, slot]).astype(jnp.int32)
+
+
+def lane_limits(contexts, lengths):
+    lane = np.arange(DL, dtype=np.int32)
+    row = np.arange(PPG, dtype=np.int32)[:, None] * HALF_GRP + lane % HALF_GRP
+    spare = (lane % DH >= STEPS * HALF_GRP)[None, :]
+    prompt = np.broadcast_to(np.arange(PPG, dtype=np.int32)[:, None], (PPG, DL))
+    limits = jnp.minimum(lookup(contexts, row), lookup(lengths, prompt))
+    return jnp.where(spare, 0, limits).reshape(PPG, 1, DL)
+
+
+def absorb_queries(q_ref, dq_ref, u_ref, qt_ref, dqt_ref):
     for p in range(PPG):
         for a in range(2):
             rows = []
@@ -121,45 +103,49 @@
         dqt_ref[p] = jnp.concatenate(rows, axis=0).T.astype(jnp.bfloat16)
 
 
-def prepare_queries(prompt_queries, decode_queries, key_up):
-    return pl.pallas_call(
-        queries_kernel,
-        out_shape=(
-            jax.ShapeDtypeStruct((UNITS, RANK, QL), jnp.bfloat16),
-            jax.ShapeDtypeStruct((PPG, RANK, DL), jnp.bfloat16),
-        ),
-        cost_estimate=pl.CostEstimate(flops=10**9, bytes_accessed=10**6, transcendentals=0),
-        name="queries",
-    )(prompt_queries, decode_queries, key_up)
-
-
-def softmax_step(s, keep, v, m_ref, l_ref, acc_ref, at):
-    s = jnp.where(keep, s * SCALE2, NEG)
+def take_scores(k, q, keep_of, s_ref, peak_ref, p):
+    s = jnp.dot(k, q, preferred_element_type=jnp.float32)
+    peak = None
+    for j in range(G):
+        rows = slice(j * BLOCK, (j + 1) * BLOCK)
+        part = jnp.where(keep_of(j), s[rows], NEG)
+        s_ref[p, rows] = part
+        top = jnp.max(part, axis=0, keepdims=True)
+        peak = top if peak is None else jnp.maximum(peak, top)
+    peak_ref[p] = peak
+
+
+def weights_of(s_ref, peak_ref, p, m_ref, l_ref, at):
     old = m_ref[at]
-    new = jnp.maximum(old, jnp.max(s, axis=0, keepdims=True))
+    new = jnp.maximum(old, peak_ref[p] * SCALE2)
     factor = jnp.exp2(old - new)
-    w = jnp.exp2(s - new)
+    total = l_ref[at] * factor
+    parts = []
+    for j in range(G):
+        w = jnp.exp2(s_ref[p, j * BLOCK : (j + 1) * BLOCK] * SCALE2 - new)
+        total = total + jnp.sum(w, axis=0, keepdims=True)
+        parts.append(w.astype(jnp.bfloat16))
     m_ref[at] = new
-    l_ref[at] = l_ref[at] * factor + jnp.sum(w, axis=0, keepdims=True)
-    w = w.astype(jnp.bfloat16)
-
-    def weigh():
-        part = lax.dot_general(v, w, (((0,), (0,)), ((), ())), preferred_element_type=jnp.float32)
-        acc_ref[at] = acc_ref[at] * factor + part
-
-    return weigh
+    l_ref[at] = total
+    return jnp.concatenate(parts, axis=0), factor
+
+
+def weigh(v, w, factor, acc_ref, at):
+    part = lax.dot_general(v, w, (((0,), (0,)), ((), ())), preferred_element_type=jnp.float32)
+    acc_ref[at] = acc_ref[at] * factor + part
 
 
 def chunk_kernel(chunk, n_src, sizes, first, last, *refs):
     refs = list(refs)
-    meta = refs.pop(0)
+    order, lengths, contexts = refs.pop(0), refs.pop(0), refs.pop(0)
     pages = refs.pop(0) if last else None
     mine = [refs.pop(0) for _ in range(n_src)]
     theirs = [refs.pop(0) for _ in range(n_src)]
-    qt, dqt, limit = refs.pop(0), refs.pop(0), refs.pop(0)
+    limit = refs.pop(0)
     if first:
-        new_mine, new_theirs = refs.pop(0), refs.pop(0)
+        new_mine, new_theirs, q_in, dq_in, key_up = [refs.pop(0) for _ in range(5)]
     else:
+        qt, dqt = refs.pop(0), refs.pop(0)
         state_in = [refs.pop(0) for _ in range(6)]
     if last:
         others = [(refs.pop(0), refs.pop(0)) for _ in range(7)]
@@ -167,7 +153,9 @@
         out_ref, dec_ref, cache_ref = refs.pop(0), refs.pop(0), refs.pop(0)
     else:
         state_out = [refs.pop(0) for _ in range(6)]
-    kbuf, vbuf, sbuf, dsbuf, offset, sems = [refs.pop(0) for _ in range(6)]
+        if first:
+            qt, dqt = refs.pop(0), refs.pop(0)
+    kbuf, vbuf, sbuf, dsbuf, peak, dpeak, offset, place, sems = [refs.pop(0) for _ in range(9)]
     if last:
         page_sems = refs.pop(0)
         state = state_in
@@ -175,7 +163,8 @@
         state = state_out
     m, l, acc, dm, dl, dacc = state
 
-    sec = meta[chunk, M_POS + 2]
+    sec, ci = lax.axis_index("sec"), lax.axis_index("cp")
+    z, y = ci // YN, lax.rem(ci, YN)
     spans, at = [], 0
     for n in sizes:
         spans.append((at, n))
@@ -199,7 +188,6 @@
             copy.start()
 
     if last:
-        z, y = meta[chunk, M_POS], meta[chunk, M_POS + 1]
         table = [(0, dy, others[0][0].at[dy], others[0][1].at[dy]) for dy in range(YN)]
         for i, dz in enumerate([7, 1, 6, 2, 5, 3]):
             table += [(dz, dy, others[1 + i][0].at[dy], others[1 + i][1].at[dy]) for dy in range(YN)]
@@ -234,7 +222,36 @@
                 one.start()
                 two.start()
 
+    slots = [j for j in range(16) if SLOT_OK[chunk, j]]
+    orders = []
+    for j in slots:
+        source = lax.rem(z + int(SLOT_Z[chunk, j]), ZN) * YN + lax.rem(y + int(SLOT_Y[chunk, j]), YN)
+        orders.append(order[2 * source + int(SLOT_A[chunk, j])])
+    ranks = [jnp.int32(0)] * len(slots)
+    for i in range(len(slots)):
+        for j in range(i):
+            ahead = jnp.where(orders[j] < orders[i], 1, 0)
+            ranks[i], ranks[j] = ranks[i] + ahead, ranks[j] + 1 - ahead
+    for i, j in enumerate(slots):
+        place[ranks[i]] = jnp.int32(int(SLOT_ROW[chunk, j]))
+        place[16 + ranks[i]] = orders[i]
+    owns = [order[2 * ci + a] for a in range(2)]
+    longest = jnp.maximum(lengths[0], lengths[1])
+    reach = jnp.int32(0)
+    for n in range(ROW_GRP):
+        reach = jnp.maximum(reach, jnp.minimum(contexts[n], lengths[n // HALF_GRP]))
+    every = []
+    for a in range(2):
+        count = jnp.int32(0)
+        for one in orders:
+            count = count + jnp.where(one <= owns[a], 1, 0)
+        every.append(jnp.where(owns[a] * BLOCK < longest, count, 0))
+    dec_count = jnp.int32(0)
+    for one in orders:
+        dec_count = dec_count + jnp.where(one * BLOCK < reach, 1, 0)
+
     if first:
+        absorb_queries(q_in, dq_in, key_up, qt, dqt)
         m[...] = jnp.full(m.shape, NEG, jnp.float32)
         l[...] = jnp.zeros(l.shape, jnp.float32)
         acc[...] = jnp.zeros(acc.shape, jnp.float32)
@@ -251,9 +268,9 @@
                 values.append(jnp.concatenate([v] * (DL // HALF_GRP), axis=0).T)
                 s = jnp.sum(dqt[p].astype(jnp.float32) * k, axis=0, keepdims=True) * SCALE2
                 scores.append(jnp.where(t <= step_of, s, NEG))
-            peak = jnp.maximum(jnp.maximum(scores[0], scores[1]), scores[2])
-            weights = [jnp.exp2(s - peak) for s in scores]
-            dm[p] = peak
+            top = jnp.maximum(jnp.maximum(scores[0], scores[1]), scores[2])
+            weights = [jnp.exp2(s - top) for s in scores]
+            dm[p] = top
             dl[p] = weights[0] + weights[1] + weights[2]
             total = jnp.zeros((RANK, DL), jnp.float32)
             for w, v in zip(weights, values):
@@ -267,12 +284,12 @@
         copy.wait()
 
     def rows_of(buf, g, p):
-        return jnp.concatenate([buf[meta[chunk, M_IDX + g * G + j] + 2 * p] for j in range(G)], axis=0)
+        return jnp.concatenate([buf[place[g * G + j] + 2 * p] for j in range(G)], axis=0)
 
     key_row = lax.broadcasted_iota(jnp.int32, (BLOCK, QL), 0)
     query_row = lax.rem(lax.broadcasted_iota(jnp.int32, (BLOCK, QL), 1), BLOCK)
     offset[...] = key_row - query_row
-    groups = [(meta[chunk, M_ALL + a] + G - 1) // G for a in range(2)]
+    groups = [(every[a] + G - 1) // G for a in range(2)]
     work = groups[0] + groups[1]
 
     def part_of(w):
@@ -281,7 +298,12 @@
 
     def scores(w, p):
         a, g = part_of(w)
-        sbuf[p] = jnp.dot(rows_of(kbuf, g, p), qt[2 * p + a], preferred_element_type=jnp.float32)
+        own = jnp.where(a == 0, owns[0], owns[1])
+
+        def keep_of(j):
+            return offset[...] <= (own - place[16 + g * G + j]) * BLOCK
+
+        take_scores(rows_of(kbuf, g, p), qt[2 * p + a], keep_of, sbuf, peak, p)
 
     @pl.when(work > 0)
     def _():
@@ -290,24 +312,23 @@
 
     def step(w, carry):
         a, g = part_of(w)
-        own = meta[chunk, M_OWN + a]
-        keep = jnp.concatenate(
-            [offset[...] <= (own - meta[chunk, M_ORD + g * G + j]) * BLOCK for j in range(G)], axis=0
-        )
         after = jnp.minimum(w + 1, work - 1)
         for p in range(PPG):
-            weigh = softmax_step(sbuf[p], keep, rows_of(vbuf, g, p), m, l, acc, 2 * p + a)
+            weights, factor = weights_of(sbuf, peak, p, m, l, 2 * p + a)
             scores(after, p)
-            weigh()
+            weigh(rows_of(vbuf, g, p), weights, factor, acc, 2 * p + a)
         return carry
 
     lax.fori_loop(0, work, step, 0)
 
     dec_row = lax.broadcasted_iota(jnp.int32, (BLOCK, DL), 0)
-    dec_work = (meta[chunk, M_DEC] + G - 1) // G
+    dec_work = (dec_count + G - 1) // G
 
     def dec_scores(g, p):
-        dsbuf[p] = jnp.dot(rows_of(kbuf, g, p), dqt[p], preferred_element_type=jnp.float32)
+        def keep_of(j):
+            return dec_row < limit[p] - place[16 + g * G + j] * BLOCK
+
+        take_scores(rows_of(kbuf, g, p), dqt[p], keep_of, dsbuf, dpeak, p)
 
     @pl.when(dec_work > 0)
     def _():
@@ -317,12 +338,9 @@
     def dec_step(g, carry):
         after = jnp.minimum(g + 1, dec_work - 1)
         for p in range(PPG):
-            keep = jnp.concatenate(
-                [dec_row < limit[p] - meta[chunk, M_ORD + g * G + j] * BLOCK for j in range(G)], axis=0
-            )
-            weigh = softmax_step(dsbuf[p], keep, rows_of(vbuf, g, p), dm, dl, dacc, p)
+            weights, factor = weights_of(dsbuf, dpeak, p, dm, dl, p)
             dec_scores(after, p)
-            weigh()
+            weigh(rows_of(vbuf, g, p), weights, factor, dacc, p)
         return carry
 
     lax.fori_loop(0, dec_work, dec_step, 0)
@@ -332,8 +350,8 @@
         for p in range(PPG):
             for a in range(2):
                 at = p * 2 + a
-                o = (acc[at] / l[at]).T.astype(jnp.bfloat16)
-                live = row + meta[chunk, M_OWN + a] * BLOCK < meta[chunk, M_LEN + p]
+                o = (acc[at] * (1.0 / l[at])).T.astype(jnp.bfloat16)
+                live = row + owns[a] * BLOCK < lengths[p]
                 for h in range(HEADS):
                     cols = slice(h * HEAD, (h + 1) * HEAD)
                     r = jnp.dot(
@@ -342,7 +360,7 @@
                     out_ref[p, a * BLOCK : (a + 1) * BLOCK, cols] = jnp.where(live, r, 0.0).astype(
                         jnp.bfloat16
                     )
-            o = (dacc[p] / dl[p]).T.astype(jnp.bfloat16)
+            o = (dacc[p] * (1.0 / dl[p])).T.astype(jnp.bfloat16)
             for h in range(HEADS):
                 cols = slice(h * HEAD, (h + 1) * HEAD)
                 r = jnp.dot(
@@ -369,28 +387,37 @@
 )
 
 
-def attend_chunk(chunk, meta, mine, theirs, qt, dqt, limit, state=None, new=None, ending=None):
+QUERIES = (
+    jax.ShapeDtypeStruct((UNITS, RANK, QL), jnp.bfloat16),
+    jax.ShapeDtypeStruct((PPG, RANK, DL), jnp.bfloat16),
+)
+
+
+def attend_chunk(chunk, control, mine, theirs, limit, queries=None, state=None, start=None, ending=None):
     first, last = state is None, ending is not None
     smem, vmem = pl.BlockSpec(memory_space=pltpu.SMEM), pl.BlockSpec(memory_space=pltpu.VMEM)
     anywhere = pl.BlockSpec(memory_space=pl.ANY)
     sizes = [a.size // (BLOCK * RANK) for a in mine]
     flat = [a.reshape(-1, BLOCK, RANK) for a in [*mine, *theirs]]
-    args, specs = [meta], [smem]
+    args, specs = list(control), [smem] * 3
     if last:
         args, specs = args + [ending["pages"]], specs + [smem]
     args, specs = args + flat, specs + [anywhere] * len(flat)
-    args, specs = args + [qt, dqt, limit], specs + [vmem] * 3
+    args, specs = args + [limit], specs + [vmem]
     if first:
-        args, specs = args + list(new), specs + [vmem] * 2
+        args, specs = args + list(start), specs + [vmem] * 5
     else:
-        args, specs = args + list(state), specs + [vmem] * 6
+        args, specs = args + list(queries) + list(state), specs + [vmem] * 8
     rows = sum(sizes)
     scratch = [
         pltpu.VMEM((rows, BLOCK, RANK), jnp.bfloat16),
         pltpu.VMEM((rows, BLOCK, RANK), jnp.bfloat16),
         pltpu.VMEM((PPG, GK, QL), jnp.float32),
         pltpu.VMEM((PPG, GK, DL), jnp.float32),
+        pltpu.VMEM((PPG, 1, QL), jnp.float32),
+        pltpu.VMEM((PPG, 1, DL), jnp.float32),
         pltpu.VMEM((BLOCK, QL), jnp.int32),
+        pltpu.SMEM((32,), jnp.int32),
         pltpu.SemaphoreType.DMA((2 * len(mine),)),
     ]
     if last:
@@ -404,7 +431,7 @@
         )
         scratch.append(pltpu.SemaphoreType.DMA((2 * CP,)))
     else:
-        shapes = STATE
+        shapes = STATE + QUERIES if first else STATE
     work = rows * BLOCK * (2 * QL + DL) * RANK * 4
     return pl.pallas_call(
         functools.partial(chunk_kernel, chunk, len(mine), sizes, first, last),
@@ -413,7 +440,7 @@
         out_specs=[vmem] * len(shapes),
         scratch_shapes=scratch,
         cost_estimate=pl.CostEstimate(flops=2 * work, bytes_accessed=4 * 10**6, transcendentals=work // 512),
-        compiler_params=pltpu.CompilerParams(vmem_limit_bytes=48 * 2**20),
+        compiler_params=pltpu.CompilerParams(vmem_limit_bytes=20 * 2**20),
     )(*args)
 
 
@@ -442,7 +469,7 @@
     decode_context,
 ):
     width = prompt_states.shape[-1]
-    ci, sec = lax.axis_index("cp"), lax.axis_index("sec")
+    ci = lax.axis_index("cp")
     own = jnp.dot(
         prompt_states.reshape(PPG * 2 * BLOCK, width), latent_down, preferred_element_type=jnp.float32
     )
@@ -450,16 +477,16 @@
     new = jnp.dot(
         decode_states.reshape(STEPS * ROW_GRP, width), latent_down, preferred_element_type=jnp.float32
     ).astype(jnp.bfloat16)
-    meta, pages, limit = scalar_tables(
-        block_order, prompt_lengths, decode_context, page_owner[0], ci, sec
-    )
-    qt, dqt = prepare_queries(prompt_queries, decode_queries, key_up)
+    control = (block_order, prompt_lengths, decode_context)
+    pages = page_table(page_owner[0], ci)
+    limit = lane_limits(decode_context, prompt_lengths)
 
     plane = jnp.stack([own, shifted(own, 0, -1), shifted(own, 0, 2), shifted(own, 0, 1)])
     new_far = swapped(new)
     up, down = shifted(plane, 1, 0), shifted(plane, -1, 0)
     plane_far = swapped(plane)
-    state = attend_chunk(0, meta, [plane], [plane_far], qt, dqt, limit, new=(new, new_far))
+    start = (new, new_far, prompt_queries, decode_queries, key_up)
+    *state, qt, dqt = attend_chunk(0, control, [plane], [plane_far], limit, start=start)
     others = [(plane, plane_far)]
     for c in range(1, 4):
         if c < 3:
@@ -470,11 +497,15 @@
             down_next = shifted(down[2:], -1, 0)
         up_far, down_far = swapped(up), swapped(down)
         others += [(up, up_far), (down, down_far)]
-        state = attend_chunk(c, meta, [up, down], [up_far, down_far], qt, dqt, limit, state=state)
+        state = attend_chunk(
+            c, control, [up, down], [up_far, down_far], limit, queries=(qt, dqt), state=state
+        )
         up, down = up_next, down_next
     ending = dict(pages=pages, others=others, value_up=value_up)
     far = [swapped(up), swapped(down)]
-    prefill_out, decode_out, cache = attend_chunk(4, meta, [up, down], far, qt, dqt, limit, state=state, ending=ending)
+    prefill_out, decode_out, cache = attend_chunk(
+        4, control, [up, down], far, limit, queries=(qt, dqt), state=state, ending=ending
+    )
     return prefill_out, decode_out, cache.reshape(1, 1, PAGES_DEV * PAGE, 2 * RANK)
 
 

time: 103 us -> 90.1 us (0.87)
  Pallas kernels: 49.3 us -> 38.3 us
  waiting for transfers between devices: 12 us -> 15.7 us
  local copies, waits for them, and re-layouts: 5.62 us -> 2.65 us
  other arithmetic: 5.28 us -> 2.41 us
    pallas_call x5, Pallas kernels: 46.7 us -> 38.3 us  [attend_chunk(): pl.pallas_call(functools.partial(chunk_kernel, chunk, len(mine), sizes, f...]
    ppermute x11, waiting for transfers between devices: 11.9 us -> 15.7 us  [shifted(): return lax.ppermute(x, 'cp', pairs)]
    pallas_call x1 -> x0, Pallas kernels: 2.53 us -> none  [prepare_queries(): pl.pallas_call(queries_kernel, out_shape=(jax.ShapeDtypeStruct((UNITS, RA...]
    reduce_max x2 -> x0, other arithmetic: 2.53 us -> none  [the longest x1 1.93 us: scalar_tables(): dec = jnp.sum(order * BLOCK < jnp.max(limits), axis=-1, keepdims=True)]
    unnamed x42 -> x20, local copies, waits for them, and re-layouts: 4.48 us -> 2.62 us
  transfers between devices with their start and end apart: 21 -> 21, of which waited for: 3 -> 5; matrix products, arithmetic and copies ran while one was open for 7% -> 3% of each run, Pallas kernels for 39% -> 33%
where the time goes in v1:
time: 90.1 us; the launch traced here: 89.8 us
  Pallas kernels  38.3 us (43%)
  starting transfers between devices  24.4 us (27%)
  waiting for transfers between devices  15.7 us (17%)
  matrix products  5.3 us (6%)
  local copies, waits for them, and re-layouts  2.65 us (3%)
  other arithmetic  2.41 us (3%)
  between operations  1.01 us (1%)
    pallas_call x5, Pallas kernels, attend_chunk(): pl.pallas_call(functools.partial(chunk_kernel, chunk, len(mine), sizes, f...  38.3 us
    ppermute x11, waiting for transfers between devices, shifted(): return lax.ppermute(x, 'cp', pairs)  15.7 us
    ppermute x11, starting transfers between devices, shifted(): return lax.ppermute(x, 'cp', pairs)  14.8 us
    ppermute x10, starting transfers between devices, swapped(): return lax.ppermute(x, 'sec', [(0, 1), (1, 0)])  9.66 us
    dot_general x1, matrix products, body(): jnp.dot(prompt_states.reshape(PPG * 2 * BLOCK, width), latent_down, prefe...  4.68 us
    unnamed x20, local copies, waits for them, and re-layouts  2.62 us
  transfers between devices with their start and end apart: 21, of which 5 were waited for; matrix products, arithmetic and copies ran while one was open for 3% of the time, Pallas kernels for 33%

profile of v1, /device:TPU:129, one launch (start us, length us, event | category | flops | bytes accessed | tf_op | source)
XLA Modules:
  0.0 89.8 jit_solution(5787590426749962376)
XLA Ops:
  0.6 1.6 %copy-done = bf16[8192,128]{1,0:T(8,128)(2,1)S(1)} copy-done((bf16[8192,128]{1,0:T(8,128)(2,1)S(1)}, bf16[8192,128]{1,0:T(8,128)(2,1)}, u32[]{:S(2)}) %copy-start) | copy-done | bytes 2097176
  2.2 4.7 %convolution_convert_fusion = bf16[384,128]{1,0:T(8,128)(2,1)S(1)} fusion(bf16[384,8192]{1,0:T(8,128)(2,1)} %bitcast.54, bf16[8192,128]{1,0:T(8,128)(2,1)S(1)} %copy-done), kind=kOutput, calls=%fused_computation | convolution fusion | flops 805355520 | bytes 8486912 | tf_op jit(solution)/shard_map/dot_general | solution.py:473
  6.9 2.8 %collective-permute-start = (bf16[4,96,128]{2,1,0:T(8,128)(2,1)S(1)}, bf16[4,96,128]{2,1,0:T(8,128)(2,1)S(1)}, u32[]{:S(2)}, u32[]{:S(2)}) collective-permute-start(bf16[4,96,128]{2,1,0:T(8,128)(2,1)S(1)} %bitcast.56), channel_id=1, source_target_pairs={{0,3},{1,0},{2,1},{3,2},{4,7},{5,4},{6,5},{7,6},{8,11},{9,8},{10,9... | collective-permute-start | bytes 294920 | tf_op jit(solution)/shard_map/ppermute | solution.py:451
  11.4 3.4 %collective-permute-done.1 = bf16[4,96,128]{2,1,0:T(8,128)(2,1)S(1)} collective-permute-done((bf16[4,96,128]{2,1,0:T(8,128)(2,1)S(1)}, bf16[4,96,128]{2,1,0:T(8,128)(2,1)S(1)}, u32[]{:S(2)}, u32[]{:S(2)}) %collective-permute-start.1) | collective-permute-done | bytes 98336 | tf_op jit(solution)/shard_map/ppermute | solution.py:451
  14.8 2.8 %collective-permute-done.2 = bf16[4,96,128]{2,1,0:T(8,128)(2,1)S(1)} collective-permute-done((bf16[4,96,128]{2,1,0:T(8,128)(2,1)S(1)}, bf16[4,96,128]{2,1,0:T(8,128)(2,1)S(1)}, u32[]{:S(2)}, u32[]{:S(2)}) %collective-permute-start.2) | collective-permute-done | bytes 98336 | tf_op jit(solution)/shard_map/ppermute | solution.py:451
  17.7 0.8 collective-permute-start.3
  18.5 1.9 %collective-permute-start.7 = (bf16[4,4,96,128]{3,2,1,0:T(8,128)(2,1)S(1)}, bf16[4,4,96,128]{3,2,1,0:T(8,128)(2,1)S(1)}, u32[]{:S(2)}, u32[]{:S(2)}) collective-permute-start(bf16[4,4,96,128]{3,2,1,0:T(8,128)(2,1)S(1)} %pad_maximum_fusion.refs_17_), channel_id=1, source_target_pairs={{0,28},{1,29},{2,30},{3,31},{4,0},{5,1},{6,2},{7,3},{8,4},{9,5},{1... | collective-permute-start | bytes 1179656 | tf_op jit(solution)/shard_map/ppermute | solution.py:451
  21.1 1.6 %collective-permute-start.14 = (bf16[96,128]{1,0:T(8,128)(2,1)S(1)}, bf16[96,128]{1,0:T(8,128)(2,1)}, u32[]{:S(2)}, u32[]{:S(2)}) collective-permute-start(bf16[96,128]{1,0:T(8,128)(2,1)S(1)} %convolution_convert_fusion.1.refs_6_), channel_id=1, source_target_pairs={{0,128},{128,0},{1,129},{129,1},{2,130},{130,2},{3,131},{131,3},{4... | collective-permute-start | bytes 73736 | tf_op jit(solution)/shard_map/ppermute | solution.py:455
  22.7 6.1 %collective-permute-done.3.refs_19_ = bf16[4,4,96,128]{3,2,1,0:T(8,128)(2,1)S(1)} collective-permute-done((bf16[4,4,96,128]{3,2,1,0:T(8,128)(2,1)S(1)}, bf16[4,4,96,128]{3,2,1,0:T(8,128)(2,1)S(1)}, u32[]{:S(2)}, u32[]{:S(2)}) %collective-permute-start.3) | collective-permute-done | bytes 393248 | tf_op jit(solution)/shard_map/ppermute | solution.py:451
  28.8 2.7 %collective-permute-start.8 = (bf16[4,4,96,128]{3,2,1,0:T(8,128)(2,1)S(1)}, bf16[4,4,96,128]{3,2,1,0:T(8,128)(2,1)S(1)}, u32[]{:S(2)}, u32[]{:S(2)}) collective-permute-start(bf16[4,4,96,128]{3,2,1,0:T(8,128)(2,1)S(1)} %collective-permute-done.7.refs_21_), channel_id=1, source_target_pairs={{0,28},{1,29},{2,30},{3,31},{4,0},{5,1},{6,2},{7,3},{8,4},{9,5},{1... | collective-permute-start | bytes 1179656 | tf_op jit(solution)/shard_map/ppermute | solution.py:451
  31.6 0.8 select_reduce_fusion
  32.3 2.4 %collective-permute-start.13 = (bf16[4,4,96,128]{3,2,1,0:T(8,128)(2,1)S(1)}, bf16[4,4,96,128]{3,2,1,0:T(8,128)(2,1)S(1)}, u32[]{:S(2)}, u32[]{:S(2)}) collective-permute-start(bf16[4,4,96,128]{3,2,1,0:T(8,128)(2,1)S(1)} %pad_maximum_fusion.refs_17_), channel_id=1, source_target_pairs={{0,128},{128,0},{1,129},{129,1},{2,130},{130,2},{3,131},{131,3},{4... | collective-permute-start | bytes 1179656 | tf_op jit(solution)/shard_map/ppermute | solution.py:455
  34.9 0.8 select_reduce_fusion.1
  36.2 2.7 %collective-permute-done.4.refs_23_ = bf16[4,4,96,128]{3,2,1,0:T(8,128)(2,1)S(1)} collective-permute-done((bf16[4,4,96,128]{3,2,1,0:T(8,128)(2,1)S(1)}, bf16[4,4,96,128]{3,2,1,0:T(8,128)(2,1)S(1)}, u32[]{:S(2)}, u32[]{:S(2)}) %collective-permute-start.4) | collective-permute-done | bytes 393248 | tf_op jit(solution)/shard_map/ppermute | solution.py:451
  38.9 2.7 %collective-permute-start.9 = (bf16[4,4,96,128]{3,2,1,0:T(8,128)(2,1)S(1)}, bf16[4,4,96,128]{3,2,1,0:T(8,128)(2,1)S(1)}, u32[]{:S(2)}, u32[]{:S(2)}) collective-permute-start(bf16[4,4,96,128]{3,2,1,0:T(8,128)(2,1)S(1)} %collective-permute-done.8.refs_25_), channel_id=1, source_target_pairs={{0,28},{1,29},{2,30},{3,31},{4,0},{5,1},{6,2},{7,3},{8,4},{9,5},{1... | collective-permute-start | bytes 1179656 | tf_op jit(solution)/shard_map/ppermute | solution.py:451
  42.2 3.2 %collective-permute-start.17 = (bf16[4,4,96,128]{3,2,1,0:T(8,128)(2,1)S(1)}, bf16[4,4,96,128]{3,2,1,0:T(8,128)(2,1)S(1)}, u32[]{:S(2)}, u32[]{:S(2)}) collective-permute-start(bf16[4,4,96,128]{3,2,1,0:T(8,128)(2,1)S(1)} %collective-permute-done.4.refs_23_), channel_id=1, source_target_pairs={{0,128},{128,0},{1,129},{129,1},{2,130},{130,2},{3,131},{131,3},{4... | collective-permute-start | bytes 1179656 | tf_op jit(solution)/shard_map/ppermute | solution.py:455
  45.7 1.0 %copy-done.5 = bf16[2,192,512]{2,1,0:T(8,128)(2,1)S(1)} copy-done((bf16[2,192,512]{2,1,0:T(8,128)(2,1)S(1)}, bf16[2,192,512]{2,1,0:T(8,128)(2,1)}, u32[]{:S(2)}) %copy-start.5) | copy-done | bytes 393240
  46.7 5.5 %shard_map.178 = (f32[4,1,384]{2,1,0:T(1,128)S(1)}, f32[4,1,384]{2,1,0:T(1,128)S(1)}, f32[4,128,384]{2,1,0:T(8,128)S(1)}, f32[2,1,256]{2,1,0:T(1,128)S(1)}, f32[...) custom-call(s32[64]{0:T(128)S(1)} %copy-done.4, ...), custom_call_target="tpu_custom_call" | custom-call | flops 1610612736 | bytes 4000000 | tf_op jit(solution)/shard_map/pallas_call | solution.py:436
  52.8 8.1 %shard_map.179 = (f32[4,1,384]{2,1,0:T(1,128)S(1)}, f32[4,1,384]{2,1,0:T(1,128)S(1)}, f32[4,128,384]{2,1,0:T(8,128)S(1)}, f32[2,1,256]{2,1,0:T(1,128)S(1)}, f32[...) custom-call(s32[64]{0:T(128)S(1)} %copy-done.4, s32[2]{0:T(128)S(1)} %copy-done.2, s32[32]{0:T(128)S(1)} %copy-done.3, ...), custom_call_target="tpu_custom_call" | custom-call | flops 3221225472 | bytes 4000000 | tf_op jit(solution)/shard_map/pallas_call | solution.py:436
  61.1 2.7 %collective-permute-start.10 = (bf16[2,4,96,128]{3,2,1,0:T(8,128)(2,1)S(1)}, bf16[2,4,96,128]{3,2,1,0:T(8,128)(2,1)S(1)}, u32[]{:S(2)}, u32[]{:S(2)}) collective-permute-start(bf16[2,4,96,128]{3,2,1,0:T(8,128)(2,1)S(1)} %slice.9), channel_id=1, source_target_pairs={{0,28},{1,29},{2,30},{3,31},{4,0},{5,1},{6,2},{7,3},{8,4},{9,5},{1... | collective-permute-start | bytes 589832 | tf_op jit(solution)/shard_map/ppermute | solution.py:451
  63.8 8.1 %shard_map.180 = (f32[4,1,384]{2,1,0:T(1,128)S(1)}, f32[4,1,384]{2,1,0:T(1,128)S(1)}, f32[4,128,384]{2,1,0:T(8,128)S(1)}, f32[2,1,256]{2,1,0:T(1,128)S(1)}, f32[...) custom-call(s32[64]{0:T(128)S(1)} %copy-done.4, s32[2]{0:T(128)S(1)} %copy-done.2, s32[32]{0:T(128)S(1)} %copy-done.3, ...), custom_call_target="tpu_custom_call" | custom-call | flops 3221225472 | bytes 4000000 | tf_op jit(solution)/shard_map/pallas_call | solution.py:436
  72.0 0.9 collective-permute-start.11
  73.0 8.2 %shard_map.181 = (f32[4,1,384]{2,1,0:T(1,128)S(1)}, f32[4,1,384]{2,1,0:T(1,128)S(1)}, f32[4,128,384]{2,1,0:T(8,128)S(1)}, f32[2,1,256]{2,1,0:T(1,128)S(1)}, f32[...) custom-call(s32[64]{0:T(128)S(1)} %copy-done.4, s32[2]{0:T(128)S(1)} %copy-done.2, s32[32]{0:T(128)S(1)} %copy-done.3, ...), custom_call_target="tpu_custom_call" | custom-call | flops 3221225472 | bytes 4000000 | tf_op jit(solution)/shard_map/pallas_call | solution.py:436
  81.2 8.4 %shard_map.182 = (bf16[2,192,512]{2,1,0:T(8,128)(2,1)}, bf16[3,32,512]{2,1,0:T(8,128)(2,1)}, bf16[384,256]{1,0:T(8,128)(2,1)}) custom-call(s32[64]{0:T(128)S(1)} %copy-done.4, s32[2]{0:T(128)S(1)} %copy-done.2, s32[32]{0:T(128)S(1)} %copy-done.3, s32[3,32]{1,0:T(4,128)S(1)} %pad_add_fusion.refs_3_, bf16[8,96,128]{2,1,0:T(8,128)(2,1)S(1)} %bitcast.50, ...), custom_call_target="tpu_custom_call" | custom-call | flops 1610612736 | bytes 4000000 | tf_op jit(solution)/shard_map/pallas_call | solution.py:436
  (55 shorter events, 4.9 us)
Async XLA Ops:
  6.9 4.5 %collective-permute-start = (bf16[4,96,128]{2,1,0:T(8,128)(2,1)S(1)}, bf16[4,96,128]{2,1,0:T(8,128)(2,1)S(1)}, u32[]{:S(2)}, u32[]{:S(2)}) collective-permute-start(bf16[4,96,128]{2,1,0:T(8,128)(2,1)S(1)} %bitcast.56), channel_id=1, source_target_pairs={{0,3},{1,0},{2,1},{3,2},{4,7},{5,4},{6,5},{7,6},{8,11},{9,8},{10,9... | collective-permute-start | bytes 294920 | tf_op jit(solution)/shard_map/ppermute | solution.py:451
  9.7 5.1 %collective-permute-start.1 = (bf16[4,96,128]{2,1,0:T(8,128)(2,1)S(1)}, bf16[4,96,128]{2,1,0:T(8,128)(2,1)S(1)}, u32[]{:S(2)}, u32[]{:S(2)}) collective-permute-start(bf16[4,96,128]{2,1,0:T(8,128)(2,1)S(1)} %bitcast.57), channel_id=1, source_target_pairs={{0,2},{1,3},{2,0},{3,1},{4,6},{5,7},{6,4},{7,5},{8,10},{9,11},{10,... | collective-permute-start | bytes 294920 | tf_op jit(solution)/shard_map/ppermute | solution.py:451
  10.1 7.5 %collective-permute-start.2 = (bf16[4,96,128]{2,1,0:T(8,128)(2,1)S(1)}, bf16[4,96,128]{2,1,0:T(8,128)(2,1)S(1)}, u32[]{:S(2)}, u32[]{:S(2)}) collective-permute-start(bf16[4,96,128]{2,1,0:T(8,128)(2,1)S(1)} %bitcast.58), channel_id=1, source_target_pairs={{0,1},{1,2},{2,3},{3,0},{4,5},{5,6},{6,7},{7,4},{8,9},{9,10},{10,1... | collective-permute-start | bytes 294920 | tf_op jit(solution)/shard_map/ppermute | solution.py:451
  17.6 28.1 %copy-start.4 = (s32[64]{0:T(128)S(1)}, s32[64]{0:T(128)}, u32[]{:S(2)}) copy-start(s32[64]{0:T(128)} %refs_0_.9) | copy-start | bytes 772
  17.6 28.1 %copy-start.6 = (bf16[128,512]{1,0:T(8,128)(2,1)S(1)}, bf16[128,512]{1,0:T(8,128)(2,1)}, u32[]{:S(2)}) copy-start(bf16[128,512]{1,0:T(8,128)(2,1)} %refs_10_.1) | copy-start | bytes 393220
  17.7 28.1 %copy-start.7 = (bf16[3,32,512]{2,1,0:T(8,128)(2,1)S(1)}, bf16[3,32,512]{2,1,0:T(8,128)(2,1)}, u32[]{:S(2)}) copy-start(bf16[3,32,512]{2,1,0:T(8,128)(2,1)} %refs_9_.1) | copy-start | bytes 294916
  17.7 11.0 %collective-permute-start.3 = (bf16[4,4,96,128]{3,2,1,0:T(8,128)(2,1)S(1)}, bf16[4,4,96,128]{3,2,1,0:T(8,128)(2,1)S(1)}, u32[]{:S(2)}, u32[]{:S(2)}) collective-permute-start(bf16[4,4,96,128]{3,2,1,0:T(8,128)(2,1)S(1)} %pad_maximum_fusion.refs_17_), channel_id=1, source_target_pairs={{0,4},{1,5},{2,6},{3,7},{4,8},{5,9},{6,10},{7,11},{8,12},{9,13},{1... | collective-permute-start | bytes 1179656 | tf_op jit(solution)/shard_map/ppermute | solution.py:451
  18.5 10.2 %collective-permute-start.7 = (bf16[4,4,96,128]{3,2,1,0:T(8,128)(2,1)S(1)}, bf16[4,4,96,128]{3,2,1,0:T(8,128)(2,1)S(1)}, u32[]{:S(2)}, u32[]{:S(2)}) collective-permute-start(bf16[4,4,96,128]{3,2,1,0:T(8,128)(2,1)S(1)} %pad_maximum_fusion.refs_17_), channel_id=1, source_target_pairs={{0,28},{1,29},{2,30},{3,31},{4,0},{5,1},{6,2},{7,3},{8,4},{9,5},{1... | collective-permute-start | bytes 1179656 | tf_op jit(solution)/shard_map/ppermute | solution.py:451
  21.1 14.5 %collective-permute-start.14 = (bf16[96,128]{1,0:T(8,128)(2,1)S(1)}, bf16[96,128]{1,0:T(8,128)(2,1)}, u32[]{:S(2)}, u32[]{:S(2)}) collective-permute-start(bf16[96,128]{1,0:T(8,128)(2,1)S(1)} %convolution_convert_fusion.1.refs_6_), channel_id=1, source_target_pairs={{0,128},{128,0},{1,129},{129,1},{2,130},{130,2},{3,131},{131,3},{4... | collective-permute-start | bytes 73736 | tf_op jit(solution)/shard_map/ppermute | solution.py:455
  28.8 10.1 %collective-permute-start.4 = (bf16[4,4,96,128]{3,2,1,0:T(8,128)(2,1)S(1)}, bf16[4,4,96,128]{3,2,1,0:T(8,128)(2,1)S(1)}, u32[]{:S(2)}, u32[]{:S(2)}) collective-permute-start(bf16[4,4,96,128]{3,2,1,0:T(8,128)(2,1)S(1)} %collective-permute-done.3.refs_19_), channel_id=1, source_target_pairs={{0,4},{1,5},{2,6},{3,7},{4,8},{5,9},{6,10},{7,11},{8,12},{9,13},{1... | collective-permute-start | bytes 1179656 | tf_op jit(solution)/shard_map/ppermute | solution.py:451
  28.8 10.1 %collective-permute-start.8 = (bf16[4,4,96,128]{3,2,1,0:T(8,128)(2,1)S(1)}, bf16[4,4,96,128]{3,2,1,0:T(8,128)(2,1)S(1)}, u32[]{:S(2)}, u32[]{:S(2)}) collective-permute-start(bf16[4,4,96,128]{3,2,1,0:T(8,128)(2,1)S(1)} %collective-permute-done.7.refs_21_), channel_id=1, source_target_pairs={{0,28},{1,29},{2,30},{3,31},{4,0},{5,1},{6,2},{7,3},{8,4},{9,5},{1... | collective-permute-start | bytes 1179656 | tf_op jit(solution)/shard_map/ppermute | solution.py:451
  32.3 9.9 %collective-permute-start.13 = (bf16[4,4,96,128]{3,2,1,0:T(8,128)(2,1)S(1)}, bf16[4,4,96,128]{3,2,1,0:T(8,128)(2,1)S(1)}, u32[]{:S(2)}, u32[]{:S(2)}) collective-permute-start(bf16[4,4,96,128]{3,2,1,0:T(8,128)(2,1)S(1)} %pad_maximum_fusion.refs_17_), channel_id=1, source_target_pairs={{0,128},{128,0},{1,129},{129,1},{2,130},{130,2},{3,131},{131,3},{4... | collective-permute-start | bytes 1179656 | tf_op jit(solution)/shard_map/ppermute | solution.py:455
  34.8 10.7 %collective-permute-start.19 = (bf16[4,4,96,128]{3,2,1,0:T(8,128)(2,1)S(1)}, bf16[4,4,96,128]{3,2,1,0:T(8,128)(2,1)S(1)}, u32[]{:S(2)}, u32[]{:S(2)}) collective-permute-start(bf16[4,4,96,128]{3,2,1,0:T(8,128)(2,1)S(1)} %collective-permute-done.3.refs_19_), channel_id=1, source_target_pairs={{0,128},{128,0},{1,129},{129,1},{2,130},{130,2},{3,131},{131,3},{4... | collective-permute-start | bytes 1179656 | tf_op jit(solution)/shard_map/ppermute | solution.py:455
  35.7 17.2 %collective-permute-start.20 = (bf16[4,4,96,128]{3,2,1,0:T(8,128)(2,1)S(1)}, bf16[4,4,96,128]{3,2,1,0:T(8,128)(2,1)S(1)}, u32[]{:S(2)}, u32[]{:S(2)}) collective-permute-start(bf16[4,4,96,128]{3,2,1,0:T(8,128)(2,1)S(1)} %collective-permute-done.7.refs_21_), channel_id=1, source_target_pairs={{0,128},{128,0},{1,129},{129,1},{2,130},{130,2},{3,131},{131,3},{4... | collective-permute-start | bytes 1179656 | tf_op jit(solution)/shard_map/ppermute | solution.py:455
  38.9 13.3 %collective-permute-start.5 = (bf16[4,4,96,128]{3,2,1,0:T(8,128)(2,1)S(1)}, bf16[4,4,96,128]{3,2,1,0:T(8,128)(2,1)S(1)}, u32[]{:S(2)}, u32[]{:S(2)}) collective-permute-start(bf16[4,4,96,128]{3,2,1,0:T(8,128)(2,1)S(1)} %collective-permute-done.4.refs_23_), channel_id=1, source_target_pairs={{0,4},{1,5},{2,6},{3,7},{4,8},{5,9},{6,10},{7,11},{8,12},{9,13},{1... | collective-permute-start | bytes 1179656 | tf_op jit(solution)/shard_map/ppermute | solution.py:451
  38.9 13.7 %collective-permute-start.9 = (bf16[4,4,96,128]{3,2,1,0:T(8,128)(2,1)S(1)}, bf16[4,4,96,128]{3,2,1,0:T(8,128)(2,1)S(1)}, u32[]{:S(2)}, u32[]{:S(2)}) collective-permute-start(bf16[4,4,96,128]{3,2,1,0:T(8,128)(2,1)S(1)} %collective-permute-done.8.refs_25_), channel_id=1, source_target_pairs={{0,28},{1,29},{2,30},{3,31},{4,0},{5,1},{6,2},{7,3},{8,4},{9,5},{1... | collective-permute-start | bytes 1179656 | tf_op jit(solution)/shard_map/ppermute | solution.py:451
  42.2 18.9 %collective-permute-start.17 = (bf16[4,4,96,128]{3,2,1,0:T(8,128)(2,1)S(1)}, bf16[4,4,96,128]{3,2,1,0:T(8,128)(2,1)S(1)}, u32[]{:S(2)}, u32[]{:S(2)}) collective-permute-start(bf16[4,4,96,128]{3,2,1,0:T(8,128)(2,1)S(1)} %collective-permute-done.4.refs_23_), channel_id=1, source_target_pairs={{0,128},{128,0},{1,129},{129,1},{2,130},{130,2},{3,131},{131,3},{4... | collective-permute-start | bytes 1179656 | tf_op jit(solution)/shard_map/ppermute | solution.py:455
  45.4 18.4 %collective-permute-start.18 = (bf16[4,4,96,128]{3,2,1,0:T(8,128)(2,1)S(1)}, bf16[4,4,96,128]{3,2,1,0:T(8,128)(2,1)S(1)}, u32[]{:S(2)}, u32[]{:S(2)}) collective-permute-start(bf16[4,4,96,128]{3,2,1,0:T(8,128)(2,1)S(1)} %collective-permute-done.8.refs_25_), channel_id=1, source_target_pairs={{0,128},{128,0},{1,129},{129,1},{2,130},{130,2},{3,131},{131,3},{4... | collective-permute-start | bytes 1179656 | tf_op jit(solution)/shard_map/ppermute | solution.py:455
  52.2 20.8 %collective-permute-start.15 = (bf16[4,4,96,128]{3,2,1,0:T(8,128)(2,1)S(1)}, bf16[4,4,96,128]{3,2,1,0:T(8,128)(2,1)S(1)}, u32[]{:S(2)}, u32[]{:S(2)}) collective-permute-start(bf16[4,4,96,128]{3,2,1,0:T(8,128)(2,1)S(1)} %collective-permute-done.5.refs_27_), channel_id=1, source_target_pairs={{0,128},{128,0},{1,129},{129,1},{2,130},{130,2},{3,131},{131,3},{4... | collective-permute-start | bytes 1179656 | tf_op jit(solution)/shard_map/ppermute | solution.py:455
  52.5 20.5 %collective-permute-start.16 = (bf16[4,4,96,128]{3,2,1,0:T(8,128)(2,1)S(1)}, bf16[4,4,96,128]{3,2,1,0:T(8,128)(2,1)S(1)}, u32[]{:S(2)}, u32[]{:S(2)}) collective-permute-start(bf16[4,4,96,128]{3,2,1,0:T(8,128)(2,1)S(1)} %collective-permute-done.9.refs_29_), channel_id=1, source_target_pairs={{0,128},{128,0},{1,129},{129,1},{2,130},{130,2},{3,131},{131,3},{4... | collective-permute-start | bytes 1179656 | tf_op jit(solution)/shard_map/ppermute | solution.py:455
  61.0 11.0 %collective-permute-start.6 = (bf16[2,4,96,128]{3,2,1,0:T(8,128)(2,1)S(1)}, bf16[2,4,96,128]{3,2,1,0:T(8,128)(2,1)S(1)}, u32[]{:S(2)}, u32[]{:S(2)}) collective-permute-start(bf16[2,4,96,128]{3,2,1,0:T(8,128)(2,1)S(1)} %slice.8), channel_id=1, source_target_pairs={{0,4},{1,5},{2,6},{3,7},{4,8},{5,9},{6,10},{7,11},{8,12},{9,13},{1... | collective-permute-start | bytes 589832 | tf_op jit(solution)/shard_map/ppermute | solution.py:451
  61.1 11.8 %collective-permute-start.10 = (bf16[2,4,96,128]{3,2,1,0:T(8,128)(2,1)S(1)}, bf16[2,4,96,128]{3,2,1,0:T(8,128)(2,1)S(1)}, u32[]{:S(2)}, u32[]{:S(2)}) collective-permute-start(bf16[2,4,96,128]{3,2,1,0:T(8,128)(2,1)S(1)} %slice.9), channel_id=1, source_target_pairs={{0,28},{1,29},{2,30},{3,31},{4,0},{5,1},{6,2},{7,3},{8,4},{9,5},{1... | collective-permute-start | bytes 589832 | tf_op jit(solution)/shard_map/ppermute | solution.py:451
  72.0 9.2 %collective-permute-start.11 = (bf16[2,4,96,128]{3,2,1,0:T(8,128)(2,1)S(1)}, bf16[2,4,96,128]{3,2,1,0:T(8,128)(2,1)S(1)}, u32[]{:S(2)}, u32[]{:S(2)}) collective-permute-start(bf16[2,4,96,128]{3,2,1,0:T(8,128)(2,1)S(1)} %collective-permute-done.6), channel_id=1, source_target_pairs={{0,128},{128,0},{1,129},{129,1},{2,130},{130,2},{3,131},{131,3},{4... | collective-permute-start | bytes 589832 | tf_op jit(solution)/shard_map/ppermute | solution.py:455
  72.9 8.3 %collective-permute-start.12 = (bf16[2,4,96,128]{3,2,1,0:T(8,128)(2,1)S(1)}, bf16[2,4,96,128]{3,2,1,0:T(8,128)(2,1)S(1)}, u32[]{:S(2)}, u32[]{:S(2)}) collective-permute-start(bf16[2,4,96,128]{3,2,1,0:T(8,128)(2,1)S(1)} %collective-permute-done.10), channel_id=1, source_target_pairs={{0,128},{128,0},{1,129},{129,1},{2,130},{130,2},{3,131},{131,3},{4... | collective-permute-start | bytes 589832 | tf_op jit(solution)/shard_map/ppermute | solution.py:455
  (7 other events, 70.6 us)

commit v2 on v1

--- a/solution.py
+++ b/solution.py
@@ -138,7 +138,7 @@
 def chunk_kernel(chunk, n_src, sizes, first, last, *refs):
     refs = list(refs)
     order, lengths, contexts = refs.pop(0), refs.pop(0), refs.pop(0)
-    pages = refs.pop(0) if last else None
+    pages = refs.pop(0)
     mine = [refs.pop(0) for _ in range(n_src)]
     theirs = [refs.pop(0) for _ in range(n_src)]
     limit = refs.pop(0)
@@ -148,16 +148,19 @@
         qt, dqt = refs.pop(0), refs.pop(0)
         state_in = [refs.pop(0) for _ in range(6)]
     if last:
-        others = [(refs.pop(0), refs.pop(0)) for _ in range(7)]
         vup = refs.pop(0)
-        out_ref, dec_ref, cache_ref = refs.pop(0), refs.pop(0), refs.pop(0)
+    if not first:
+        refs.pop(0)
+    if last:
+        out_ref, dec_ref = refs.pop(0), refs.pop(0)
     else:
         state_out = [refs.pop(0) for _ in range(6)]
         if first:
             qt, dqt = refs.pop(0), refs.pop(0)
+    cache_ref = refs.pop(0)
     kbuf, vbuf, sbuf, dsbuf, peak, dpeak, offset, place, sems = [refs.pop(0) for _ in range(9)]
-    if last:
-        page_sems = refs.pop(0)
+    page_sems = refs.pop(0)
+    if last:
         state = state_in
     else:
         state = state_out
@@ -187,40 +190,31 @@
         for copy in copies(theirs, mine):
             copy.start()
 
-    if last:
-        table = [(0, dy, others[0][0].at[dy], others[0][1].at[dy]) for dy in range(YN)]
-        for i, dz in enumerate([7, 1, 6, 2, 5, 3]):
-            table += [(dz, dy, others[1 + i][0].at[dy], others[1 + i][1].at[dy]) for dy in range(YN)]
-        for i in range(2):
-            table += [(4, 2 * i + e, mine[i].at[pl.ds(e * 4, 4)], theirs[i].at[pl.ds(e * 4, 4)]) for e in range(2)]
-
-        def page_copies(n, dz, dy, own_src, far_src):
-            s = lax.rem(z + dz, ZN) * YN + lax.rem(y + dy, YN)
-            page, slot = pages[PG_K, s], pages[PG_SLOT, s]
-            block, row = page // 6, pl.multiple_of(lax.rem(page, 6) * PAGE, PAGE)
-            rows = pl.ds(pl.multiple_of(jnp.minimum(slot, PAGES_DEV - 1) * PAGE, PAGE), PAGE)
-            own_at, far_at = sec * RANK, (1 - sec) * RANK
-            return (
-                pages[PG_HAS, s] > 0,
-                pltpu.make_async_copy(
-                    own_src.at[block, pl.ds(row, PAGE), :],
-                    cache_ref.at[rows, pl.ds(pl.multiple_of(own_at, RANK), RANK)],
-                    page_sems.at[2 * n],
-                ),
-                pltpu.make_async_copy(
-                    far_src.at[block, pl.ds(row, PAGE), :],
-                    cache_ref.at[rows, pl.ds(pl.multiple_of(far_at, RANK), RANK)],
-                    page_sems.at[2 * n + 1],
-                ),
-            )
-
-        for n, entry in enumerate(table):
-            has, one, two = page_copies(n, *entry)
-
-            @pl.when(has)
-            def _(one=one, two=two):
-                one.start()
-                two.start()
+    sources = []
+    for i, dz in enumerate(CHUNK_Z[chunk]):
+        sources += [(dz, dy, i, 4 * dy) for dy in range(YN)]
+    if last:
+        sources = [(4, 2 * i + e, i, 4 * e) for i in range(2) for e in range(2)]
+
+    def page_copies(n, dz, dy, i, base):
+        s = lax.rem(z + dz, ZN) * YN + lax.rem(y + dy, YN)
+        page, slot = pages[PG_K, s], pages[PG_SLOT, s]
+        block = base + page // 6
+        row = pl.ds(pl.multiple_of(lax.rem(page, 6) * PAGE, PAGE), PAGE)
+        rows = pl.ds(pl.multiple_of(jnp.minimum(slot, PAGES_DEV - 1) * PAGE, PAGE), PAGE)
+        made = []
+        for src, half, at in ((mine[i], sec, 2 * n), (theirs[i], 1 - sec, 2 * n + 1)):
+            cols = pl.ds(pl.multiple_of(half * RANK, RANK), RANK)
+            made.append(pltpu.make_async_copy(src.at[block, row, :], cache_ref.at[rows, cols], page_sems.at[at]))
+        return pages[PG_HAS, s] > 0, made
+
+    for n, entry in enumerate(sources):
+        has, made = page_copies(n, *entry)
+
+        @pl.when(has)
+        def _(made=made):
+            for copy in made:
+                copy.start()
 
     slots = [j for j in range(16) if SLOT_OK[chunk, j]]
     orders = []
@@ -368,13 +362,14 @@
                 ).astype(jnp.bfloat16)
                 for t in range(STEPS):
                     dec_ref[t, p * HALF_GRP : (p + 1) * HALF_GRP, cols] = r[t * HALF_GRP : (t + 1) * HALF_GRP]
-        for n, entry in enumerate(table):
-            has, one, two = page_copies(n, *entry)
-
-            @pl.when(has)
-            def _(one=one, two=two):
-                one.wait()
-                two.wait()
+
+    for n, entry in enumerate(sources):
+        has, made = page_copies(n, *entry)
+
+        @pl.when(has)
+        def _(made=made):
+            for copy in made:
+                copy.wait()
 
 
 STATE = (
@@ -393,21 +388,24 @@
 )
 
 
-def attend_chunk(chunk, control, mine, theirs, limit, queries=None, state=None, start=None, ending=None):
-    first, last = state is None, ending is not None
+def attend_chunk(chunk, control, mine, theirs, limit, queries=None, state=None, start=None, value_up=None):
+    first, last = state is None, value_up is not None
     smem, vmem = pl.BlockSpec(memory_space=pltpu.SMEM), pl.BlockSpec(memory_space=pltpu.VMEM)
     anywhere = pl.BlockSpec(memory_space=pl.ANY)
     sizes = [a.size // (BLOCK * RANK) for a in mine]
     flat = [a.reshape(-1, BLOCK, RANK) for a in [*mine, *theirs]]
-    args, specs = list(control), [smem] * 3
-    if last:
-        args, specs = args + [ending["pages"]], specs + [smem]
+    args, specs = list(control), [smem] * 4
     args, specs = args + flat, specs + [anywhere] * len(flat)
     args, specs = args + [limit], specs + [vmem]
     if first:
         args, specs = args + list(start), specs + [vmem] * 5
     else:
+        *state, cache = state
         args, specs = args + list(queries) + list(state), specs + [vmem] * 8
+    if last:
+        args, specs = args + [value_up], specs + [vmem]
+    if not first:
+        args, specs = args + [cache], specs + [anywhere]
     rows = sum(sizes)
     scratch = [
         pltpu.VMEM((rows, BLOCK, RANK), jnp.bfloat16),
@@ -420,28 +418,65 @@
         pltpu.SMEM((32,), jnp.int32),
         pltpu.SemaphoreType.DMA((2 * len(mine),)),
     ]
-    if last:
-        for pair in ending["others"]:
-            args, specs = args + list(pair), specs + [anywhere] * 2
-        args, specs = args + [ending["value_up"]], specs + [vmem]
+    scratch.append(pltpu.SemaphoreType.DMA((2 * (2 * rows // 8),)))
+    if last:
         shapes = (
             jax.ShapeDtypeStruct((PPG, 2 * BLOCK, HEADS * HEAD), jnp.bfloat16),
             jax.ShapeDtypeStruct((STEPS, ROW_GRP, HEADS * HEAD), jnp.bfloat16),
-            jax.ShapeDtypeStruct((PAGES_DEV * PAGE, 2 * RANK), jnp.bfloat16),
         )
-        scratch.append(pltpu.SemaphoreType.DMA((2 * CP,)))
     else:
         shapes = STATE + QUERIES if first else STATE
+    out_specs = [vmem] * len(shapes) + [anywhere]
+    shapes += (jax.ShapeDtypeStruct((PAGES_DEV * PAGE, 2 * RANK), jnp.bfloat16),)
     work = rows * BLOCK * (2 * QL + DL) * RANK * 4
     return pl.pallas_call(
         functools.partial(chunk_kernel, chunk, len(mine), sizes, first, last),
         out_shape=shapes,
         in_specs=specs,
-        out_specs=[vmem] * len(shapes),
+        out_specs=out_specs,
         scratch_shapes=scratch,
+        input_output_aliases={} if first else {len(args) - 1: len(shapes) - 1},
         cost_estimate=pl.CostEstimate(flops=2 * work, bytes_accessed=4 * 10**6, transcendentals=work // 512),
         compiler_params=pltpu.CompilerParams(vmem_limit_bytes=20 * 2**20),
     )(*args)
+
+
+def project_kernel(x_ref, w_ref, out_ref, total):
+    k = pl.program_id(0)
+    part = jnp.dot(x_ref[...], w_ref[...], preferred_element_type=jnp.float32)
+
+    @pl.when(k == 0)
+    def _():
+        total[...] = part
+
+    @pl.when(k > 0)
+    def _():
+        total[...] += part
+
+    @pl.when(k == pl.num_programs(0) - 1)
+    def _():
+        out_ref[...] = total[...].astype(jnp.bfloat16)
+
+
+def project(x, w, parts=8):
+    rows, width = x.shape
+    depth = width // parts
+    return pl.pallas_call(
+        project_kernel,
+        grid=(parts,),
+        out_shape=jax.ShapeDtypeStruct((rows, RANK), jnp.bfloat16),
+        in_specs=[
+            pl.BlockSpec((rows, depth), lambda k: (0, k)),
+            pl.BlockSpec((depth, RANK), lambda k: (k, 0)),
+        ],
+        out_specs=pl.BlockSpec((rows, RANK), lambda k: (0, 0)),
+        scratch_shapes=[pltpu.VMEM((rows, RANK), jnp.float32)],
+        cost_estimate=pl.CostEstimate(
+            flops=2 * rows * width * RANK, bytes_accessed=2 * width * (rows + RANK), transcendentals=0
+        ),
+        compiler_params=pltpu.CompilerParams(vmem_limit_bytes=8 * 2**20),
+        name="project",
+    )(x, w)
 
 
 def shifted(x, dz, dy):
@@ -470,15 +505,12 @@
 ):
     width = prompt_states.shape[-1]
     ci = lax.axis_index("cp")
-    own = jnp.dot(
-        prompt_states.reshape(PPG * 2 * BLOCK, width), latent_down, preferred_element_type=jnp.float32
-    )
-    own = own.astype(jnp.bfloat16).reshape(UNITS, BLOCK, RANK)
+    own = project(prompt_states.reshape(PPG * 2 * BLOCK, width), latent_down)
+    own = own.reshape(UNITS, BLOCK, RANK)
     new = jnp.dot(
         decode_states.reshape(STEPS * ROW_GRP, width), latent_down, preferred_element_type=jnp.float32
     ).astype(jnp.bfloat16)
-    control = (block_order, prompt_lengths, decode_context)
-    pages = page_table(page_owner[0], ci)
+    control = (block_order, prompt_lengths, decode_context, page_table(page_owner[0], ci))
     limit = lane_limits(decode_context, prompt_lengths)
 
     plane = jnp.stack([own, shifted(own, 0, -1), shifted(own, 0, 2), shifted(own, 0, 1)])
@@ -486,8 +518,8 @@
     up, down = shifted(plane, 1, 0), shifted(plane, -1, 0)
     plane_far = swapped(plane)
     start = (new, new_far, prompt_queries, decode_queries, key_up)
-    *state, qt, dqt = attend_chunk(0, control, [plane], [plane_far], limit, start=start)
-    others = [(plane, plane_far)]
+    *state, qt, dqt, cache = attend_chunk(0, control, [plane], [plane_far], limit, start=start)
+    state = [*state, cache]
     for c in range(1, 4):
         if c < 3:
             up_next = shifted(up, 1, 0)
@@ -496,15 +528,13 @@
             up_next = shifted(up[:2], 1, 0)
             down_next = shifted(down[2:], -1, 0)
         up_far, down_far = swapped(up), swapped(down)
-        others += [(up, up_far), (down, down_far)]
         state = attend_chunk(
             c, control, [up, down], [up_far, down_far], limit, queries=(qt, dqt), state=state
         )
         up, down = up_next, down_next
-    ending = dict(pages=pages, others=others, value_up=value_up)
     far = [swapped(up), swapped(down)]
     prefill_out, decode_out, cache = attend_chunk(
-        4, control, [up, down], far, limit, queries=(qt, dqt), state=state, ending=ending
+        4, control, [up, down], far, limit, queries=(qt, dqt), state=state, value_up=value_up
     )
     return prefill_out, decode_out, cache.reshape(1, 1, PAGES_DEV * PAGE, 2 * RANK)
 

time: 90.1 us -> 90.7 us (level)
  the two profiles are of different devices: /device:TPU:129 before, /device:TPU:1 now
where the time goes in v2:
time: 90.7 us; the launch traced here: 89.5 us
  Pallas kernels  34.8 us (38%)
  starting transfers between devices  30 us (33%)
  waiting for transfers between devices  18.1 us (20%)
  local copies, waits for them, and re-layouts  4.58 us (5%)
  between operations  1.06 us (1%)
    pallas_call x5, Pallas kernels, attend_chunk(): pl.pallas_call(functools.partial(chunk_kernel, chunk, len(mine), sizes, f...  31.1 us
    ppermute x11, starting transfers between devices, shifted(): return lax.ppermute(x, 'cp', pairs)  20.7 us
    ppermute x11, waiting for transfers between devices, shifted(): return lax.ppermute(x, 'cp', pairs)  18.1 us
    ppermute x10, starting transfers between devices, swapped(): return lax.ppermute(x, 'sec', [(0, 1), (1, 0)])  9.35 us
    unnamed x28, local copies, waits for them, and re-layouts  4.55 us
    pallas_call x1, Pallas kernels, project(): pl.pallas_call(project_kernel, grid=(parts,), out_shape=jax.ShapeDtypeStr...  3.65 us
  transfers between devices with their start and end apart: 21, of which 5 were waited for; matrix products, arithmetic and copies ran while one was open for 1% of the time, Pallas kernels for 28%

profile of v2, /device:TPU:1, one launch (start us, length us, event | category | flops | bytes accessed | tf_op | source)
XLA Modules:
  0.0 89.5 jit_solution(3363551616838780108)
XLA Ops:
  0.7 1.7 %copy-done.1 = bf16[8192,128]{1,0:T(8,128)(2,1)S(1)} copy-done((bf16[8192,128]{1,0:T(8,128)(2,1)S(1)}, bf16[8192,128]{1,0:T(8,128)(2,1)}, u32[]{:S(2)}) %copy-start.1) | copy-done | bytes 2097176
  2.4 2.8 %copy-done.2 = bf16[2,192,8192]{2,1,0:T(8,128)(2,1)S(1)} copy-done((bf16[2,192,8192]{2,1,0:T(8,128)(2,1)S(1)}, bf16[2,192,8192]{2,1,0:T(8,128)(2,1)}, u32[]{:S(2)}) %copy-start.2) | copy-done | bytes 6291480
  5.1 3.6 %project.1 = bf16[384,128]{1,0:T(8,128)(2,1)S(1)} custom-call(bf16[384,8192]{1,0:T(8,128)(2,1)S(1)} %bitcast.35, bf16[8192,128]{1,0:T(8,128)(2,1)S(1)} %copy-done.1), custom_call_target="tpu_custom_call" | custom-call | flops 805306368 | bytes 8388608 | tf_op jit(solution)/shard_map/project/pallas_call | solution.py:464
  8.8 3.6 %collective-permute-start = (bf16[4,96,128]{2,1,0:T(8,128)(2,1)S(1)}, bf16[4,96,128]{2,1,0:T(8,128)(2,1)S(1)}, u32[]{:S(2)}, u32[]{:S(2)}) collective-permute-start(bf16[4,96,128]{2,1,0:T(8,128)(2,1)S(1)} %bitcast.36), channel_id=1, source_target_pairs={{0,3},{1,0},{2,1},{3,2},{4,7},{5,4},{6,5},{7,6},{8,11},{9,8},{10,9... | collective-permute-start | bytes 294920 | tf_op jit(solution)/shard_map/ppermute | solution.py:486
  12.8 0.7 collective-permute-start.2
  13.5 0.6 collective-permute-done
  14.1 3.4 %collective-permute-done.1 = bf16[4,96,128]{2,1,0:T(8,128)(2,1)S(1)} collective-permute-done((bf16[4,96,128]{2,1,0:T(8,128)(2,1)S(1)}, bf16[4,96,128]{2,1,0:T(8,128)(2,1)S(1)}, u32[]{:S(2)}, u32[]{:S(2)}) %collective-permute-start.1) | collective-permute-done | bytes 98336 | tf_op jit(solution)/shard_map/ppermute | solution.py:486
  17.5 2.8 %collective-permute-done.2 = bf16[4,96,128]{2,1,0:T(8,128)(2,1)S(1)} collective-permute-done((bf16[4,96,128]{2,1,0:T(8,128)(2,1)S(1)}, bf16[4,96,128]{2,1,0:T(8,128)(2,1)S(1)}, u32[]{:S(2)}, u32[]{:S(2)}) %collective-permute-start.2) | collective-permute-done | bytes 98336 | tf_op jit(solution)/shard_map/ppermute | solution.py:486
  20.5 1.7 %collective-permute-start.3 = (bf16[4,4,96,128]{3,2,1,0:T(8,128)(2,1)S(1)}, bf16[4,4,96,128]{3,2,1,0:T(8,128)(2,1)S(1)}, u32[]{:S(2)}, u32[]{:S(2)}) collective-permute-start(bf16[4,4,96,128]{3,2,1,0:T(8,128)(2,1)S(1)} %pad_maximum_fusion), channel_id=1, source_target_pairs={{0,4},{1,5},{2,6},{3,7},{4,8},{5,9},{6,10},{7,11},{8,12},{9,13},{1... | collective-permute-start | bytes 1179656 | tf_op jit(solution)/shard_map/ppermute | solution.py:486
  22.2 4.0 %collective-permute-start.7 = (bf16[4,4,96,128]{3,2,1,0:T(8,128)(2,1)S(1)}, bf16[4,4,96,128]{3,2,1,0:T(8,128)(2,1)S(1)}, u32[]{:S(2)}, u32[]{:S(2)}) collective-permute-start(bf16[4,4,96,128]{3,2,1,0:T(8,128)(2,1)S(1)} %pad_maximum_fusion), channel_id=1, source_target_pairs={{0,28},{1,29},{2,30},{3,31},{4,0},{5,1},{6,2},{7,3},{8,4},{9,5},{1... | collective-permute-start | bytes 1179656 | tf_op jit(solution)/shard_map/ppermute | solution.py:486
  26.8 1.3 %collective-permute-start.14 = (bf16[96,128]{1,0:T(8,128)(2,1)S(1)}, bf16[96,128]{1,0:T(8,128)(2,1)S(1)}, u32[]{:S(2)}, u32[]{:S(2)}) collective-permute-start(bf16[96,128]{1,0:T(8,128)(2,1)S(1)} %convolution_convert_fusion.refs_7_), channel_id=1, source_target_pairs={{0,128},{128,0},{1,129},{129,1},{2,130},{130,2},{3,131},{131,3},{4... | collective-permute-start | bytes 73736 | tf_op jit(solution)/shard_map/ppermute | solution.py:490
  28.1 6.6 %collective-permute-done.3 = bf16[4,4,96,128]{3,2,1,0:T(8,128)(2,1)S(1)} collective-permute-done((bf16[4,4,96,128]{3,2,1,0:T(8,128)(2,1)S(1)}, bf16[4,4,96,128]{3,2,1,0:T(8,128)(2,1)S(1)}, u32[]{:S(2)}, u32[]{:S(2)}) %collective-permute-start.3) | collective-permute-done | bytes 393248 | tf_op jit(solution)/shard_map/ppermute | solution.py:486
  34.7 2.7 %collective-permute-start.8 = (bf16[4,4,96,128]{3,2,1,0:T(8,128)(2,1)S(1)}, bf16[4,4,96,128]{3,2,1,0:T(8,128)(2,1)S(1)}, u32[]{:S(2)}, u32[]{:S(2)}) collective-permute-start(bf16[4,4,96,128]{3,2,1,0:T(8,128)(2,1)S(1)} %collective-permute-done.7), channel_id=1, source_target_pairs={{0,28},{1,29},{2,30},{3,31},{4,0},{5,1},{6,2},{7,3},{8,4},{9,5},{1... | collective-permute-start | bytes 1179656 | tf_op jit(solution)/shard_map/ppermute | solution.py:486
  37.6 2.1 %collective-permute-start.13 = (bf16[4,4,96,128]{3,2,1,0:T(8,128)(2,1)S(1)}, bf16[4,4,96,128]{3,2,1,0:T(8,128)(2,1)S(1)}, u32[]{:S(2)}, u32[]{:S(2)}) collective-permute-start(bf16[4,4,96,128]{3,2,1,0:T(8,128)(2,1)S(1)} %pad_maximum_fusion), channel_id=1, source_target_pairs={{0,128},{128,0},{1,129},{129,1},{2,130},{130,2},{3,131},{131,3},{4... | collective-permute-start | bytes 1179656 | tf_op jit(solution)/shard_map/ppermute | solution.py:490
  40.4 4.6 %collective-permute-done.4 = bf16[4,4,96,128]{3,2,1,0:T(8,128)(2,1)S(1)} collective-permute-done((bf16[4,4,96,128]{3,2,1,0:T(8,128)(2,1)S(1)}, bf16[4,4,96,128]{3,2,1,0:T(8,128)(2,1)S(1)}, u32[]{:S(2)}, u32[]{:S(2)}) %collective-permute-start.4) | collective-permute-done | bytes 393248 | tf_op jit(solution)/shard_map/ppermute | solution.py:486
  45.1 2.7 %collective-permute-start.9 = (bf16[4,4,96,128]{3,2,1,0:T(8,128)(2,1)S(1)}, bf16[4,4,96,128]{3,2,1,0:T(8,128)(2,1)S(1)}, u32[]{:S(2)}, u32[]{:S(2)}) collective-permute-start(bf16[4,4,96,128]{3,2,1,0:T(8,128)(2,1)S(1)} %collective-permute-done.8), channel_id=1, source_target_pairs={{0,28},{1,29},{2,30},{3,31},{4,0},{5,1},{6,2},{7,3},{8,4},{9,5},{1... | collective-permute-start | bytes 1179656 | tf_op jit(solution)/shard_map/ppermute | solution.py:486
  47.8 3.0 %collective-permute-start.17 = (bf16[4,4,96,128]{3,2,1,0:T(8,128)(2,1)S(1)}, bf16[4,4,96,128]{3,2,1,0:T(8,128)(2,1)S(1)}, u32[]{:S(2)}, u32[]{:S(2)}) collective-permute-start(bf16[4,4,96,128]{3,2,1,0:T(8,128)(2,1)S(1)} %collective-permute-done.4), channel_id=1, source_target_pairs={{0,128},{128,0},{1,129},{129,1},{2,130},{130,2},{3,131},{131,3},{4... | collective-permute-start | bytes 1179656 | tf_op jit(solution)/shard_map/ppermute | solution.py:490
  50.9 5.2 %shard_map.178 = (f32[4,1,384]{2,1,0:T(1,128)S(1)}, f32[4,1,384]{2,1,0:T(1,128)S(1)}, f32[4,128,384]{2,1,0:T(8,128)S(1)}, f32[2,1,256]{2,1,0:T(1,128)S(1)}, f32[...) custom-call(s32[64]{0:T(128)S(1)} %copy-done.9, ...), custom_call_target="tpu_custom_call" | custom-call | flops 1610612736 | bytes 4000000 | tf_op jit(solution)/shard_map/pallas_call | solution.py:432
  56.2 1.6 %collective-permute-start.15 = (bf16[4,4,96,128]{3,2,1,0:T(8,128)(2,1)S(1)}, bf16[4,4,96,128]{3,2,1,0:T(8,128)(2,1)S(1)}, u32[]{:S(2)}, u32[]{:S(2)}) collective-permute-start(bf16[4,4,96,128]{3,2,1,0:T(8,128)(2,1)S(1)} %collective-permute-done.5), channel_id=1, source_target_pairs={{0,128},{128,0},{1,129},{129,1},{2,130},{130,2},{3,131},{131,3},{4... | collective-permute-start | bytes 1179656 | tf_op jit(solution)/shard_map/ppermute | solution.py:490
  57.8 6.6 %shard_map.179 = (f32[4,1,384]{2,1,0:T(1,128)S(1)}, f32[4,1,384]{2,1,0:T(1,128)S(1)}, f32[4,128,384]{2,1,0:T(8,128)S(1)}, f32[2,1,256]{2,1,0:T(1,128)S(1)}, f32[...) custom-call(s32[64]{0:T(128)S(1)} %copy-done.9, ...), custom_call_target="tpu_custom_call", output_to_operand_aliasing={{6}: (17, {})} | custom-call | flops 3221225472 | bytes 4000000 | tf_op jit(solution)/shard_map/pallas_call | solution.py:432
  64.5 4.8 %collective-permute-start.10 = (bf16[2,4,96,128]{3,2,1,0:T(8,128)(2,1)S(1)}, bf16[2,4,96,128]{3,2,1,0:T(8,128)(2,1)S(1)}, u32[]{:S(2)}, u32[]{:S(2)}) collective-permute-start(bf16[2,4,96,128]{3,2,1,0:T(8,128)(2,1)S(1)} %slice.9), channel_id=1, source_target_pairs={{0,28},{1,29},{2,30},{3,31},{4,0},{5,1},{6,2},{7,3},{8,4},{9,5},{1... | collective-permute-start | bytes 589832 | tf_op jit(solution)/shard_map/ppermute | solution.py:486
  69.4 6.5 %shard_map.180 = (f32[4,1,384]{2,1,0:T(1,128)S(1)}, f32[4,1,384]{2,1,0:T(1,128)S(1)}, f32[4,128,384]{2,1,0:T(8,128)S(1)}, f32[2,1,256]{2,1,0:T(1,128)S(1)}, f32[...) custom-call(s32[64]{0:T(128)S(1)} %copy-done.9, ...), custom_call_target="tpu_custom_call", output_to_operand_aliasing={{6}: (17, {})} | custom-call | flops 3221225472 | bytes 4000000 | tf_op jit(solution)/shard_map/pallas_call | solution.py:432
  76.5 7.1 %shard_map.181 = (f32[4,1,384]{2,1,0:T(1,128)S(1)}, f32[4,1,384]{2,1,0:T(1,128)S(1)}, f32[4,128,384]{2,1,0:T(8,128)S(1)}, f32[2,1,256]{2,1,0:T(1,128)S(1)}, f32[...) custom-call(s32[64]{0:T(128)S(1)} %copy-done.9, ...), custom_call_target="tpu_custom_call", output_to_operand_aliasing={{6}: (17, {})} | custom-call | flops 3221225472 | bytes 4000000 | tf_op jit(solution)/shard_map/pallas_call | solution.py:432
  83.6 5.7 %shard_map.182 = (bf16[2,192,512]{2,1,0:T(8,128)(2,1)}, bf16[3,32,512]{2,1,0:T(8,128)(2,1)}, bf16[384,256]{1,0:T(8,128)(2,1)}) custom-call(s32[64]{0:T(128)S(1)} %copy-done.9, s32[2]{0:T(128)S(1)} %copy-done.3, s32[32]{0:T(128)S(1)} %copy-done.4, s32[3,32]{1,0:T(4,128)S(1)} %pad_add_fusion.refs_3_, ...), custom_call_target="tpu_custom_call", output_to_operand_aliasing={{2}: (18, {})} | custom-call | flops 1610612736 | bytes 4000000 | tf_op jit(solution)/shard_map/pallas_call | solution.py:432
  (63 shorter events, 2.8 us)
Async XLA Ops:
  8.8 5.3 %collective-permute-start = (bf16[4,96,128]{2,1,0:T(8,128)(2,1)S(1)}, bf16[4,96,128]{2,1,0:T(8,128)(2,1)S(1)}, u32[]{:S(2)}, u32[]{:S(2)}) collective-permute-start(bf16[4,96,128]{2,1,0:T(8,128)(2,1)S(1)} %bitcast.36), channel_id=1, source_target_pairs={{0,3},{1,0},{2,1},{3,2},{4,7},{5,4},{6,5},{7,6},{8,11},{9,8},{10,9... | collective-permute-start | bytes 294920 | tf_op jit(solution)/shard_map/ppermute | solution.py:486
  12.4 5.1 %collective-permute-start.1 = (bf16[4,96,128]{2,1,0:T(8,128)(2,1)S(1)}, bf16[4,96,128]{2,1,0:T(8,128)(2,1)S(1)}, u32[]{:S(2)}, u32[]{:S(2)}) collective-permute-start(bf16[4,96,128]{2,1,0:T(8,128)(2,1)S(1)} %bitcast.37), channel_id=1, source_target_pairs={{0,2},{1,3},{2,0},{3,1},{4,6},{5,7},{6,4},{7,5},{8,10},{9,11},{10,... | collective-permute-start | bytes 294920 | tf_op jit(solution)/shard_map/ppermute | solution.py:486
  12.8 7.5 %collective-permute-start.2 = (bf16[4,96,128]{2,1,0:T(8,128)(2,1)S(1)}, bf16[4,96,128]{2,1,0:T(8,128)(2,1)S(1)}, u32[]{:S(2)}, u32[]{:S(2)}) collective-permute-start(bf16[4,96,128]{2,1,0:T(8,128)(2,1)S(1)} %bitcast.38), channel_id=1, source_target_pairs={{0,1},{1,2},{2,3},{3,0},{4,5},{5,6},{6,7},{7,4},{8,9},{9,10},{10,1... | collective-permute-start | bytes 294920 | tf_op jit(solution)/shard_map/ppermute | solution.py:486
  20.4 30.6 %copy-start.5 = (bf16[2,192,512]{2,1,0:T(8,128)(2,1)S(1)}, bf16[2,192,512]{2,1,0:T(8,128)(2,1)}, u32[]{:S(2)}) copy-start(bf16[2,192,512]{2,1,0:T(8,128)(2,1)} %refs_9_.1) | copy-start | bytes 1179652
  20.4 30.6 %copy-start.6 = (bf16[128,512]{1,0:T(8,128)(2,1)S(1)}, bf16[128,512]{1,0:T(8,128)(2,1)}, u32[]{:S(2)}) copy-start(bf16[128,512]{1,0:T(8,128)(2,1)} %refs_11_.1) | copy-start | bytes 393220
  20.4 30.6 %copy-start.8 = (bf16[3,32,512]{2,1,0:T(8,128)(2,1)S(1)}, bf16[3,32,512]{2,1,0:T(8,128)(2,1)}, u32[]{:S(2)}) copy-start(bf16[3,32,512]{2,1,0:T(8,128)(2,1)} %refs_10_.1) | copy-start | bytes 294916
  20.5 14.2 %collective-permute-start.3 = (bf16[4,4,96,128]{3,2,1,0:T(8,128)(2,1)S(1)}, bf16[4,4,96,128]{3,2,1,0:T(8,128)(2,1)S(1)}, u32[]{:S(2)}, u32[]{:S(2)}) collective-permute-start(bf16[4,4,96,128]{3,2,1,0:T(8,128)(2,1)S(1)} %pad_maximum_fusion), channel_id=1, source_target_pairs={{0,4},{1,5},{2,6},{3,7},{4,8},{5,9},{6,10},{7,11},{8,12},{9,13},{1... | collective-permute-start | bytes 1179656 | tf_op jit(solution)/shard_map/ppermute | solution.py:486
  22.2 12.5 %collective-permute-start.7 = (bf16[4,4,96,128]{3,2,1,0:T(8,128)(2,1)S(1)}, bf16[4,4,96,128]{3,2,1,0:T(8,128)(2,1)S(1)}, u32[]{:S(2)}, u32[]{:S(2)}) collective-permute-start(bf16[4,4,96,128]{3,2,1,0:T(8,128)(2,1)S(1)} %pad_maximum_fusion), channel_id=1, source_target_pairs={{0,28},{1,29},{2,30},{3,31},{4,0},{5,1},{6,2},{7,3},{8,4},{9,5},{1... | collective-permute-start | bytes 1179656 | tf_op jit(solution)/shard_map/ppermute | solution.py:486
  26.8 13.2 %collective-permute-start.14 = (bf16[96,128]{1,0:T(8,128)(2,1)S(1)}, bf16[96,128]{1,0:T(8,128)(2,1)S(1)}, u32[]{:S(2)}, u32[]{:S(2)}) collective-permute-start(bf16[96,128]{1,0:T(8,128)(2,1)S(1)} %convolution_convert_fusion.refs_7_), channel_id=1, source_target_pairs={{0,128},{128,0},{1,129},{129,1},{2,130},{130,2},{3,131},{131,3},{4... | collective-permute-start | bytes 73736 | tf_op jit(solution)/shard_map/ppermute | solution.py:490
  34.7 10.4 %collective-permute-start.4 = (bf16[4,4,96,128]{3,2,1,0:T(8,128)(2,1)S(1)}, bf16[4,4,96,128]{3,2,1,0:T(8,128)(2,1)S(1)}, u32[]{:S(2)}, u32[]{:S(2)}) collective-permute-start(bf16[4,4,96,128]{3,2,1,0:T(8,128)(2,1)S(1)} %collective-permute-done.3), channel_id=1, source_target_pairs={{0,4},{1,5},{2,6},{3,7},{4,8},{5,9},{6,10},{7,11},{8,12},{9,13},{1... | collective-permute-start | bytes 1179656 | tf_op jit(solution)/shard_map/ppermute | solution.py:486
  34.7 10.4 %collective-permute-start.8 = (bf16[4,4,96,128]{3,2,1,0:T(8,128)(2,1)S(1)}, bf16[4,4,96,128]{3,2,1,0:T(8,128)(2,1)S(1)}, u32[]{:S(2)}, u32[]{:S(2)}) collective-permute-start(bf16[4,4,96,128]{3,2,1,0:T(8,128)(2,1)S(1)} %collective-permute-done.7), channel_id=1, source_target_pairs={{0,28},{1,29},{2,30},{3,31},{4,0},{5,1},{6,2},{7,3},{8,4},{9,5},{1... | collective-permute-start | bytes 1179656 | tf_op jit(solution)/shard_map/ppermute | solution.py:486
  37.6 10.2 %collective-permute-start.13 = (bf16[4,4,96,128]{3,2,1,0:T(8,128)(2,1)S(1)}, bf16[4,4,96,128]{3,2,1,0:T(8,128)(2,1)S(1)}, u32[]{:S(2)}, u32[]{:S(2)}) collective-permute-start(bf16[4,4,96,128]{3,2,1,0:T(8,128)(2,1)S(1)} %pad_maximum_fusion), channel_id=1, source_target_pairs={{0,128},{128,0},{1,129},{129,1},{2,130},{130,2},{3,131},{131,3},{4... | collective-permute-start | bytes 1179656 | tf_op jit(solution)/shard_map/ppermute | solution.py:490
  39.7 11.1 %collective-permute-start.19 = (bf16[4,4,96,128]{3,2,1,0:T(8,128)(2,1)S(1)}, bf16[4,4,96,128]{3,2,1,0:T(8,128)(2,1)S(1)}, u32[]{:S(2)}, u32[]{:S(2)}) collective-permute-start(bf16[4,4,96,128]{3,2,1,0:T(8,128)(2,1)S(1)} %collective-permute-done.3), channel_id=1, source_target_pairs={{0,128},{128,0},{1,129},{129,1},{2,130},{130,2},{3,131},{131,3},{4... | collective-permute-start | bytes 1179656 | tf_op jit(solution)/shard_map/ppermute | solution.py:490
  39.9 17.9 %collective-permute-start.20 = (bf16[4,4,96,128]{3,2,1,0:T(8,128)(2,1)S(1)}, bf16[4,4,96,128]{3,2,1,0:T(8,128)(2,1)S(1)}, u32[]{:S(2)}, u32[]{:S(2)}) collective-permute-start(bf16[4,4,96,128]{3,2,1,0:T(8,128)(2,1)S(1)} %collective-permute-done.7), channel_id=1, source_target_pairs={{0,128},{128,0},{1,129},{129,1},{2,130},{130,2},{3,131},{131,3},{4... | collective-permute-start | bytes 1179656 | tf_op jit(solution)/shard_map/ppermute | solution.py:490
  45.1 11.1 %collective-permute-start.5 = (bf16[4,4,96,128]{3,2,1,0:T(8,128)(2,1)S(1)}, bf16[4,4,96,128]{3,2,1,0:T(8,128)(2,1)S(1)}, u32[]{:S(2)}, u32[]{:S(2)}) collective-permute-start(bf16[4,4,96,128]{3,2,1,0:T(8,128)(2,1)S(1)} %collective-permute-done.4), channel_id=1, source_target_pairs={{0,4},{1,5},{2,6},{3,7},{4,8},{5,9},{6,10},{7,11},{8,12},{9,13},{1... | collective-permute-start | bytes 1179656 | tf_op jit(solution)/shard_map/ppermute | solution.py:486
  45.1 12.7 %collective-permute-start.9 = (bf16[4,4,96,128]{3,2,1,0:T(8,128)(2,1)S(1)}, bf16[4,4,96,128]{3,2,1,0:T(8,128)(2,1)S(1)}, u32[]{:S(2)}, u32[]{:S(2)}) collective-permute-start(bf16[4,4,96,128]{3,2,1,0:T(8,128)(2,1)S(1)} %collective-permute-done.8), channel_id=1, source_target_pairs={{0,28},{1,29},{2,30},{3,31},{4,0},{5,1},{6,2},{7,3},{8,4},{9,5},{1... | collective-permute-start | bytes 1179656 | tf_op jit(solution)/shard_map/ppermute | solution.py:486
  47.8 16.7 %collective-permute-start.17 = (bf16[4,4,96,128]{3,2,1,0:T(8,128)(2,1)S(1)}, bf16[4,4,96,128]{3,2,1,0:T(8,128)(2,1)S(1)}, u32[]{:S(2)}, u32[]{:S(2)}) collective-permute-start(bf16[4,4,96,128]{3,2,1,0:T(8,128)(2,1)S(1)} %collective-permute-done.4), channel_id=1, source_target_pairs={{0,128},{128,0},{1,129},{129,1},{2,130},{130,2},{3,131},{131,3},{4... | collective-permute-start | bytes 1179656 | tf_op jit(solution)/shard_map/ppermute | solution.py:490
  50.8 18.6 %collective-permute-start.18 = (bf16[4,4,96,128]{3,2,1,0:T(8,128)(2,1)S(1)}, bf16[4,4,96,128]{3,2,1,0:T(8,128)(2,1)S(1)}, u32[]{:S(2)}, u32[]{:S(2)}) collective-permute-start(bf16[4,4,96,128]{3,2,1,0:T(8,128)(2,1)S(1)} %collective-permute-done.8), channel_id=1, source_target_pairs={{0,128},{128,0},{1,129},{129,1},{2,130},{130,2},{3,131},{131,3},{4... | collective-permute-start | bytes 1179656 | tf_op jit(solution)/shard_map/ppermute | solution.py:490
  56.2 20.3 %collective-permute-start.15 = (bf16[4,4,96,128]{3,2,1,0:T(8,128)(2,1)S(1)}, bf16[4,4,96,128]{3,2,1,0:T(8,128)(2,1)S(1)}, u32[]{:S(2)}, u32[]{:S(2)}) collective-permute-start(bf16[4,4,96,128]{3,2,1,0:T(8,128)(2,1)S(1)} %collective-permute-done.5), channel_id=1, source_target_pairs={{0,128},{128,0},{1,129},{129,1},{2,130},{130,2},{3,131},{131,3},{4... | collective-permute-start | bytes 1179656 | tf_op jit(solution)/shard_map/ppermute | solution.py:490
  57.8 18.7 %collective-permute-start.16 = (bf16[4,4,96,128]{3,2,1,0:T(8,128)(2,1)S(1)}, bf16[4,4,96,128]{3,2,1,0:T(8,128)(2,1)S(1)}, u32[]{:S(2)}, u32[]{:S(2)}) collective-permute-start(bf16[4,4,96,128]{3,2,1,0:T(8,128)(2,1)S(1)} %collective-permute-done.9), channel_id=1, source_target_pairs={{0,128},{128,0},{1,129},{129,1},{2,130},{130,2},{3,131},{131,3},{4... | collective-permute-start | bytes 1179656 | tf_op jit(solution)/shard_map/ppermute | solution.py:490
  64.4 11.5 %collective-permute-start.6 = (bf16[2,4,96,128]{3,2,1,0:T(8,128)(2,1)S(1)}, bf16[2,4,96,128]{3,2,1,0:T(8,128)(2,1)S(1)}, u32[]{:S(2)}, u32[]{:S(2)}) collective-permute-start(bf16[2,4,96,128]{3,2,1,0:T(8,128)(2,1)S(1)} %slice.8), channel_id=1, source_target_pairs={{0,4},{1,5},{2,6},{3,7},{4,8},{5,9},{6,10},{7,11},{8,12},{9,13},{1... | collective-permute-start | bytes 589832 | tf_op jit(solution)/shard_map/ppermute | solution.py:486
  64.5 11.7 %collective-permute-start.10 = (bf16[2,4,96,128]{3,2,1,0:T(8,128)(2,1)S(1)}, bf16[2,4,96,128]{3,2,1,0:T(8,128)(2,1)S(1)}, u32[]{:S(2)}, u32[]{:S(2)}) collective-permute-start(bf16[2,4,96,128]{3,2,1,0:T(8,128)(2,1)S(1)} %slice.9), channel_id=1, source_target_pairs={{0,28},{1,29},{2,30},{3,31},{4,0},{5,1},{6,2},{7,3},{8,4},{9,5},{1... | collective-permute-start | bytes 589832 | tf_op jit(solution)/shard_map/ppermute | solution.py:486
  75.9 7.7 %collective-permute-start.11 = (bf16[2,4,96,128]{3,2,1,0:T(8,128)(2,1)S(1)}, bf16[2,4,96,128]{3,2,1,0:T(8,128)(2,1)S(1)}, u32[]{:S(2)}, u32[]{:S(2)}) collective-permute-start(bf16[2,4,96,128]{3,2,1,0:T(8,128)(2,1)S(1)} %collective-permute-done.6), channel_id=1, source_target_pairs={{0,128},{128,0},{1,129},{129,1},{2,130},{130,2},{3,131},{131,3},{4... | collective-permute-start | bytes 589832 | tf_op jit(solution)/shard_map/ppermute | solution.py:490
  76.3 7.3 %collective-permute-start.12 = (bf16[2,4,96,128]{3,2,1,0:T(8,128)(2,1)S(1)}, bf16[2,4,96,128]{3,2,1,0:T(8,128)(2,1)S(1)}, u32[]{:S(2)}, u32[]{:S(2)}) collective-permute-start(bf16[2,4,96,128]{3,2,1,0:T(8,128)(2,1)S(1)} %collective-permute-done.10), channel_id=1, source_target_pairs={{0,128},{128,0},{1,129},{129,1},{2,130},{130,2},{3,131},{131,3},{4... | collective-permute-start | bytes 589832 | tf_op jit(solution)/shard_map/ppermute | solution.py:490
  (11 other events, 183.1 us)

commit v3 on v2

--- a/solution.py
+++ b/solution.py
@@ -441,44 +441,6 @@
     )(*args)
 
 
-def project_kernel(x_ref, w_ref, out_ref, total):
-    k = pl.program_id(0)
-    part = jnp.dot(x_ref[...], w_ref[...], preferred_element_type=jnp.float32)
-
-    @pl.when(k == 0)
-    def _():
-        total[...] = part
-
-    @pl.when(k > 0)
-    def _():
-        total[...] += part
-
-    @pl.when(k == pl.num_programs(0) - 1)
-    def _():
-        out_ref[...] = total[...].astype(jnp.bfloat16)
-
-
-def project(x, w, parts=8):
-    rows, width = x.shape
-    depth = width // parts
-    return pl.pallas_call(
-        project_kernel,
-        grid=(parts,),
-        out_shape=jax.ShapeDtypeStruct((rows, RANK), jnp.bfloat16),
-        in_specs=[
-            pl.BlockSpec((rows, depth), lambda k: (0, k)),
-            pl.BlockSpec((depth, RANK), lambda k: (k, 0)),
-        ],
-        out_specs=pl.BlockSpec((rows, RANK), lambda k: (0, 0)),
-        scratch_shapes=[pltpu.VMEM((rows, RANK), jnp.float32)],
-        cost_estimate=pl.CostEstimate(
-            flops=2 * rows * width * RANK, bytes_accessed=2 * width * (rows + RANK), transcendentals=0
-        ),
-        compiler_params=pltpu.CompilerParams(vmem_limit_bytes=8 * 2**20),
-        name="project",
-    )(x, w)
-
-
 def shifted(x, dz, dy):
     pairs = [
         (z * YN + y, ((z + dz) % ZN) * YN + (y + dy) % YN) for z in range(ZN) for y in range(YN)
@@ -505,8 +467,10 @@
 ):
     width = prompt_states.shape[-1]
     ci = lax.axis_index("cp")
-    own = project(prompt_states.reshape(PPG * 2 * BLOCK, width), latent_down)
-    own = own.reshape(UNITS, BLOCK, RANK)
+    own = jnp.dot(
+        prompt_states.reshape(PPG * 2 * BLOCK, width), latent_down, preferred_element_type=jnp.float32
+    )
+    own = own.astype(jnp.bfloat16).reshape(UNITS, BLOCK, RANK)
     new = jnp.dot(
         decode_states.reshape(STEPS * ROW_GRP, width), latent_down, preferred_element_type=jnp.float32
     ).astype(jnp.bfloat16)

time: 90.7 us -> 89.4 us (0.986)
  matrix products: 0.57 us -> 5.31 us
  Pallas kernels: 34.8 us -> 31.6 us
  local copies, waits for them, and re-layouts: 4.58 us -> 1.66 us
  other arithmetic: 0.38 us -> 2.41 us
  waiting for transfers between devices: 18.1 us -> 16.7 us
    dot_general x0 -> x1, matrix products: none -> 4.69 us  [body(): jnp.dot(prompt_states.reshape(PPG * 2 * BLOCK, width), latent_down, prefe...]
    pallas_call x1 -> x0, Pallas kernels: 3.65 us -> none  [project(): pl.pallas_call(project_kernel, grid=(parts,), out_shape=jax.ShapeDtypeStr...]
    unnamed x28 -> x20, local copies, waits for them, and re-layouts: 4.55 us -> 1.63 us
    ppermute x11, waiting for transfers between devices: 18.1 us -> 16.7 us  [shifted(): return lax.ppermute(x, 'cp', pairs)]
  transfers between devices with their start and end apart: 21 -> 21, of which waited for: 5 -> 5; matrix products, arithmetic and copies ran while one was open for 1% -> 3% of each run, Pallas kernels for 28% -> 29%
where the time goes in v3:
time: 89.4 us; the launch traced here: 88.1 us
  Pallas kernels  31.6 us (35%)
  starting transfers between devices  29.4 us (33%)
  waiting for transfers between devices  16.7 us (19%)
  matrix products  5.31 us (6%)
  other arithmetic  2.41 us (3%)
  local copies, waits for them, and re-layouts  1.66 us (2%)
  between operations  1.02 us (1%)
    pallas_call x5, Pallas kernels, attend_chunk(): pl.pallas_call(functools.partial(chunk_kernel, chunk, len(mine), sizes, f...  31.6 us
    ppermute x11, starting transfers between devices, shifted(): return lax.ppermute(x, 'cp', pairs)  20.7 us
    ppermute x11, waiting for transfers between devices, shifted(): return lax.ppermute(x, 'cp', pairs)  16.7 us
    ppermute x10, starting transfers between devices, swapped(): return lax.ppermute(x, 'sec', [(0, 1), (1, 0)])  8.72 us
    dot_general x1, matrix products, body(): jnp.dot(prompt_states.reshape(PPG * 2 * BLOCK, width), latent_down, prefe...  4.69 us
  transfers between devices with their start and end apart: 21, of which 5 were waited for; matrix products, arithmetic and copies ran while one was open for 3% of the time, Pallas kernels for 29%

profile of v3, /device:TPU:1, one launch (start us, length us, event | category | flops | bytes accessed | tf_op | source)
XLA Modules:
  0.0 88.1 jit_solution(743959631704881169)
XLA Ops:
  0.6 1.6 %copy-done = bf16[8192,128]{1,0:T(8,128)(2,1)S(1)} copy-done((bf16[8192,128]{1,0:T(8,128)(2,1)S(1)}, bf16[8192,128]{1,0:T(8,128)(2,1)}, u32[]{:S(2)}) %copy-start) | copy-done | bytes 2097176
  2.2 4.7 %convolution_convert_fusion = bf16[384,128]{1,0:T(8,128)(2,1)S(1)} fusion(bf16[384,8192]{1,0:T(8,128)(2,1)} %bitcast.53, bf16[8192,128]{1,0:T(8,128)(2,1)S(1)} %copy-done), kind=kOutput, calls=%fused_computation | convolution fusion | flops 805355520 | bytes 8486912 | tf_op jit(solution)/shard_map/dot_general | solution.py:470
  6.9 3.6 %collective-permute-start = (bf16[4,96,128]{2,1,0:T(8,128)(2,1)S(1)}, bf16[4,96,128]{2,1,0:T(8,128)(2,1)S(1)}, u32[]{:S(2)}, u32[]{:S(2)}) collective-permute-start(bf16[4,96,128]{2,1,0:T(8,128)(2,1)S(1)} %bitcast.55), channel_id=1, source_target_pairs={{0,3},{1,0},{2,1},{3,2},{4,7},{5,4},{6,5},{7,6},{8,11},{9,8},{10,9... | collective-permute-start | bytes 294920 | tf_op jit(solution)/shard_map/ppermute | solution.py:448
  10.9 0.7 collective-permute-start.2
  12.2 3.4 %collective-permute-done.1 = bf16[4,96,128]{2,1,0:T(8,128)(2,1)S(1)} collective-permute-done((bf16[4,96,128]{2,1,0:T(8,128)(2,1)S(1)}, bf16[4,96,128]{2,1,0:T(8,128)(2,1)S(1)}, u32[]{:S(2)}, u32[]{:S(2)}) %collective-permute-start.1) | collective-permute-done | bytes 98336 | tf_op jit(solution)/shard_map/ppermute | solution.py:448
  15.6 2.8 %collective-permute-done.2 = bf16[4,96,128]{2,1,0:T(8,128)(2,1)S(1)} collective-permute-done((bf16[4,96,128]{2,1,0:T(8,128)(2,1)S(1)}, bf16[4,96,128]{2,1,0:T(8,128)(2,1)S(1)}, u32[]{:S(2)}, u32[]{:S(2)}) %collective-permute-start.2) | collective-permute-done | bytes 98336 | tf_op jit(solution)/shard_map/ppermute | solution.py:448
  18.6 1.7 %collective-permute-start.3 = (bf16[4,4,96,128]{3,2,1,0:T(8,128)(2,1)S(1)}, bf16[4,4,96,128]{3,2,1,0:T(8,128)(2,1)S(1)}, u32[]{:S(2)}, u32[]{:S(2)}) collective-permute-start(bf16[4,4,96,128]{3,2,1,0:T(8,128)(2,1)S(1)} %pad_maximum_fusion), channel_id=1, source_target_pairs={{0,4},{1,5},{2,6},{3,7},{4,8},{5,9},{6,10},{7,11},{8,12},{9,13},{1... | collective-permute-start | bytes 1179656 | tf_op jit(solution)/shard_map/ppermute | solution.py:448
  20.3 4.0 %collective-permute-start.7 = (bf16[4,4,96,128]{3,2,1,0:T(8,128)(2,1)S(1)}, bf16[4,4,96,128]{3,2,1,0:T(8,128)(2,1)}, u32[]{:S(2)}, u32[]{:S(2)}) collective-permute-start(bf16[4,4,96,128]{3,2,1,0:T(8,128)(2,1)S(1)} %pad_maximum_fusion), channel_id=1, source_target_pairs={{0,28},{1,29},{2,30},{3,31},{4,0},{5,1},{6,2},{7,3},{8,4},{9,5},{1... | collective-permute-start | bytes 1179656 | tf_op jit(solution)/shard_map/ppermute | solution.py:448
  24.9 1.3 %collective-permute-start.14 = (bf16[96,128]{1,0:T(8,128)(2,1)S(1)}, bf16[96,128]{1,0:T(8,128)(2,1)}, u32[]{:S(2)}, u32[]{:S(2)}) collective-permute-start(bf16[96,128]{1,0:T(8,128)(2,1)S(1)} %convolution_convert_fusion.1.refs_7_), channel_id=1, source_target_pairs={{0,128},{128,0},{1,129},{129,1},{2,130},{130,2},{3,131},{131,3},{4... | collective-permute-start | bytes 73736 | tf_op jit(solution)/shard_map/ppermute | solution.py:452
  26.2 6.6 %collective-permute-done.3 = bf16[4,4,96,128]{3,2,1,0:T(8,128)(2,1)S(1)} collective-permute-done((bf16[4,4,96,128]{3,2,1,0:T(8,128)(2,1)S(1)}, bf16[4,4,96,128]{3,2,1,0:T(8,128)(2,1)S(1)}, u32[]{:S(2)}, u32[]{:S(2)}) %collective-permute-start.3) | collective-permute-done | bytes 393248 | tf_op jit(solution)/shard_map/ppermute | solution.py:448
  32.8 2.7 %collective-permute-start.8 = (bf16[4,4,96,128]{3,2,1,0:T(8,128)(2,1)}, bf16[4,4,96,128]{3,2,1,0:T(8,128)(2,1)S(1)}, u32[]{:S(2)}, u32[]{:S(2)}) collective-permute-start(bf16[4,4,96,128]{3,2,1,0:T(8,128)(2,1)} %collective-permute-done.7), channel_id=1, source_target_pairs={{0,28},{1,29},{2,30},{3,31},{4,0},{5,1},{6,2},{7,3},{8,4},{9,5},{1... | collective-permute-start | bytes 1179656 | tf_op jit(solution)/shard_map/ppermute | solution.py:448
  35.6 0.8 select_reduce_fusion
  36.4 2.1 %collective-permute-start.13 = (bf16[4,4,96,128]{3,2,1,0:T(8,128)(2,1)S(1)}, bf16[4,4,96,128]{3,2,1,0:T(8,128)(2,1)S(1)}, u32[]{:S(2)}, u32[]{:S(2)}) collective-permute-start(bf16[4,4,96,128]{3,2,1,0:T(8,128)(2,1)S(1)} %pad_maximum_fusion), channel_id=1, source_target_pairs={{0,128},{128,0},{1,129},{129,1},{2,130},{130,2},{3,131},{131,3},{4... | collective-permute-start | bytes 1179656 | tf_op jit(solution)/shard_map/ppermute | solution.py:452
  38.6 0.8 select_reduce_fusion.1
  39.9 3.3 %collective-permute-done.4 = bf16[4,4,96,128]{3,2,1,0:T(8,128)(2,1)S(1)} collective-permute-done((bf16[4,4,96,128]{3,2,1,0:T(8,128)(2,1)S(1)}, bf16[4,4,96,128]{3,2,1,0:T(8,128)(2,1)S(1)}, u32[]{:S(2)}, u32[]{:S(2)}) %collective-permute-start.4) | collective-permute-done | bytes 393248 | tf_op jit(solution)/shard_map/ppermute | solution.py:448
  43.2 2.7 %collective-permute-start.9 = (bf16[4,4,96,128]{3,2,1,0:T(8,128)(2,1)S(1)}, bf16[4,4,96,128]{3,2,1,0:T(8,128)(2,1)S(1)}, u32[]{:S(2)}, u32[]{:S(2)}) collective-permute-start(bf16[4,4,96,128]{3,2,1,0:T(8,128)(2,1)S(1)} %collective-permute-done.8), channel_id=1, source_target_pairs={{0,28},{1,29},{2,30},{3,31},{4,0},{5,1},{6,2},{7,3},{8,4},{9,5},{1... | collective-permute-start | bytes 1179656 | tf_op jit(solution)/shard_map/ppermute | solution.py:448
  46.6 2.9 %collective-permute-start.17 = (bf16[4,4,96,128]{3,2,1,0:T(8,128)(2,1)S(1)}, bf16[4,4,96,128]{3,2,1,0:T(8,128)(2,1)S(1)}, u32[]{:S(2)}, u32[]{:S(2)}) collective-permute-start(bf16[4,4,96,128]{3,2,1,0:T(8,128)(2,1)S(1)} %collective-permute-done.4), channel_id=1, source_target_pairs={{0,128},{128,0},{1,129},{129,1},{2,130},{130,2},{3,131},{131,3},{4... | collective-permute-start | bytes 1179656 | tf_op jit(solution)/shard_map/ppermute | solution.py:452
  49.8 5.2 %shard_map.178 = (f32[4,1,384]{2,1,0:T(1,128)S(1)}, f32[4,1,384]{2,1,0:T(1,128)S(1)}, f32[4,128,384]{2,1,0:T(8,128)S(1)}, f32[2,1,256]{2,1,0:T(1,128)S(1)}, f32[...) custom-call(s32[64]{0:T(128)S(1)} %copy-done.7, ...), custom_call_target="tpu_custom_call" | custom-call | flops 1610612736 | bytes 4000000 | tf_op jit(solution)/shard_map/pallas_call | solution.py:432
  55.0 0.9 %collective-permute-start.15 = (bf16[4,4,96,128]{3,2,1,0:T(8,128)(2,1)S(1)}, bf16[4,4,96,128]{3,2,1,0:T(8,128)(2,1)S(1)}, u32[]{:S(2)}, u32[]{:S(2)}) collective-permute-start(bf16[4,4,96,128]{3,2,1,0:T(8,128)(2,1)S(1)} %collective-permute-done.5), channel_id=1, source_target_pairs={{0,128},{128,0},{1,129},{129,1},{2,130},{130,2},{3,131},{131,3},{4... | collective-permute-start | bytes 1179656 | tf_op jit(solution)/shard_map/ppermute | solution.py:452
  55.9 6.8 %shard_map.179 = (f32[4,1,384]{2,1,0:T(1,128)S(1)}, f32[4,1,384]{2,1,0:T(1,128)S(1)}, f32[4,128,384]{2,1,0:T(8,128)S(1)}, f32[2,1,256]{2,1,0:T(1,128)S(1)}, f32[...) custom-call(s32[64]{0:T(128)S(1)} %copy-done.7, ...), custom_call_target="tpu_custom_call", output_to_operand_aliasing={{6}: (17, {})} | custom-call | flops 3221225472 | bytes 4000000 | tf_op jit(solution)/shard_map/pallas_call | solution.py:432
  62.9 4.8 %collective-permute-start.10 = (bf16[2,4,96,128]{3,2,1,0:T(8,128)(2,1)S(1)}, bf16[2,4,96,128]{3,2,1,0:T(8,128)(2,1)S(1)}, u32[]{:S(2)}, u32[]{:S(2)}) collective-permute-start(bf16[2,4,96,128]{3,2,1,0:T(8,128)(2,1)S(1)} %slice.9), channel_id=1, source_target_pairs={{0,28},{1,29},{2,30},{3,31},{4,0},{5,1},{6,2},{7,3},{8,4},{9,5},{1... | collective-permute-start | bytes 589832 | tf_op jit(solution)/shard_map/ppermute | solution.py:448
  67.7 6.5 %shard_map.180 = (f32[4,1,384]{2,1,0:T(1,128)S(1)}, f32[4,1,384]{2,1,0:T(1,128)S(1)}, f32[4,128,384]{2,1,0:T(8,128)S(1)}, f32[2,1,256]{2,1,0:T(1,128)S(1)}, f32[...) custom-call(s32[64]{0:T(128)S(1)} %copy-done.7, ...), custom_call_target="tpu_custom_call", output_to_operand_aliasing={{6}: (17, {})} | custom-call | flops 3221225472 | bytes 4000000 | tf_op jit(solution)/shard_map/pallas_call | solution.py:432
  74.8 7.3 %shard_map.181 = (f32[4,1,384]{2,1,0:T(1,128)S(1)}, f32[4,1,384]{2,1,0:T(1,128)S(1)}, f32[4,128,384]{2,1,0:T(8,128)S(1)}, f32[2,1,256]{2,1,0:T(1,128)S(1)}, f32[...) custom-call(s32[64]{0:T(128)S(1)} %copy-done.7, ...), custom_call_target="tpu_custom_call", output_to_operand_aliasing={{6}: (17, {})} | custom-call | flops 3221225472 | bytes 4000000 | tf_op jit(solution)/shard_map/pallas_call | solution.py:432
  82.2 5.7 %shard_map.182 = (bf16[2,192,512]{2,1,0:T(8,128)(2,1)}, bf16[3,32,512]{2,1,0:T(8,128)(2,1)}, bf16[384,256]{1,0:T(8,128)(2,1)}) custom-call(s32[64]{0:T(128)S(1)} %copy-done.7, s32[2]{0:T(128)S(1)} %copy-done.1, s32[32]{0:T(128)S(1)} %copy-done.2, s32[3,32]{1,0:T(4,128)S(1)} %pad_add_fusion.refs_3_, ...), custom_call_target="tpu_custom_call", output_to_operand_aliasing={{2}: (18, {})} | custom-call | flops 1610612736 | bytes 4000000 | tf_op jit(solution)/shard_map/pallas_call | solution.py:432
  (55 shorter events, 4.1 us)
Async XLA Ops:
  6.9 5.3 %collective-permute-start = (bf16[4,96,128]{2,1,0:T(8,128)(2,1)S(1)}, bf16[4,96,128]{2,1,0:T(8,128)(2,1)S(1)}, u32[]{:S(2)}, u32[]{:S(2)}) collective-permute-start(bf16[4,96,128]{2,1,0:T(8,128)(2,1)S(1)} %bitcast.55), channel_id=1, source_target_pairs={{0,3},{1,0},{2,1},{3,2},{4,7},{5,4},{6,5},{7,6},{8,11},{9,8},{10,9... | collective-permute-start | bytes 294920 | tf_op jit(solution)/shard_map/ppermute | solution.py:448
  10.6 5.1 %collective-permute-start.1 = (bf16[4,96,128]{2,1,0:T(8,128)(2,1)S(1)}, bf16[4,96,128]{2,1,0:T(8,128)(2,1)S(1)}, u32[]{:S(2)}, u32[]{:S(2)}) collective-permute-start(bf16[4,96,128]{2,1,0:T(8,128)(2,1)S(1)} %bitcast.56), channel_id=1, source_target_pairs={{0,2},{1,3},{2,0},{3,1},{4,6},{5,7},{6,4},{7,5},{8,10},{9,11},{10,... | collective-permute-start | bytes 294920 | tf_op jit(solution)/shard_map/ppermute | solution.py:448
  10.9 7.5 %collective-permute-start.2 = (bf16[4,96,128]{2,1,0:T(8,128)(2,1)S(1)}, bf16[4,96,128]{2,1,0:T(8,128)(2,1)S(1)}, u32[]{:S(2)}, u32[]{:S(2)}) collective-permute-start(bf16[4,96,128]{2,1,0:T(8,128)(2,1)S(1)} %bitcast.57), channel_id=1, source_target_pairs={{0,1},{1,2},{2,3},{3,0},{4,5},{5,6},{6,7},{7,4},{8,9},{9,10},{10,1... | collective-permute-start | bytes 294920 | tf_op jit(solution)/shard_map/ppermute | solution.py:448
  18.5 31.3 %copy-start.3 = (bf16[2,192,512]{2,1,0:T(8,128)(2,1)S(1)}, bf16[2,192,512]{2,1,0:T(8,128)(2,1)}, u32[]{:S(2)}) copy-start(bf16[2,192,512]{2,1,0:T(8,128)(2,1)} %refs_9_.1) | copy-start | bytes 1179652
  18.5 31.3 %copy-start.4 = (bf16[128,512]{1,0:T(8,128)(2,1)S(1)}, bf16[128,512]{1,0:T(8,128)(2,1)}, u32[]{:S(2)}) copy-start(bf16[128,512]{1,0:T(8,128)(2,1)} %refs_11_.1) | copy-start | bytes 393220
  18.5 31.3 %copy-start.6 = (bf16[3,32,512]{2,1,0:T(8,128)(2,1)S(1)}, bf16[3,32,512]{2,1,0:T(8,128)(2,1)}, u32[]{:S(2)}) copy-start(bf16[3,32,512]{2,1,0:T(8,128)(2,1)} %refs_10_.1) | copy-start | bytes 294916
  18.6 14.2 %collective-permute-start.3 = (bf16[4,4,96,128]{3,2,1,0:T(8,128)(2,1)S(1)}, bf16[4,4,96,128]{3,2,1,0:T(8,128)(2,1)S(1)}, u32[]{:S(2)}, u32[]{:S(2)}) collective-permute-start(bf16[4,4,96,128]{3,2,1,0:T(8,128)(2,1)S(1)} %pad_maximum_fusion), channel_id=1, source_target_pairs={{0,4},{1,5},{2,6},{3,7},{4,8},{5,9},{6,10},{7,11},{8,12},{9,13},{1... | collective-permute-start | bytes 1179656 | tf_op jit(solution)/shard_map/ppermute | solution.py:448
  20.3 12.5 %collective-permute-start.7 = (bf16[4,4,96,128]{3,2,1,0:T(8,128)(2,1)S(1)}, bf16[4,4,96,128]{3,2,1,0:T(8,128)(2,1)}, u32[]{:S(2)}, u32[]{:S(2)}) collective-permute-start(bf16[4,4,96,128]{3,2,1,0:T(8,128)(2,1)S(1)} %pad_maximum_fusion), channel_id=1, source_target_pairs={{0,28},{1,29},{2,30},{3,31},{4,0},{5,1},{6,2},{7,3},{8,4},{9,5},{1... | collective-permute-start | bytes 1179656 | tf_op jit(solution)/shard_map/ppermute | solution.py:448
  24.9 14.5 %collective-permute-start.14 = (bf16[96,128]{1,0:T(8,128)(2,1)S(1)}, bf16[96,128]{1,0:T(8,128)(2,1)}, u32[]{:S(2)}, u32[]{:S(2)}) collective-permute-start(bf16[96,128]{1,0:T(8,128)(2,1)S(1)} %convolution_convert_fusion.1.refs_7_), channel_id=1, source_target_pairs={{0,128},{128,0},{1,129},{129,1},{2,130},{130,2},{3,131},{131,3},{4... | collective-permute-start | bytes 73736 | tf_op jit(solution)/shard_map/ppermute | solution.py:452
  32.8 10.4 %collective-permute-start.4 = (bf16[4,4,96,128]{3,2,1,0:T(8,128)(2,1)S(1)}, bf16[4,4,96,128]{3,2,1,0:T(8,128)(2,1)S(1)}, u32[]{:S(2)}, u32[]{:S(2)}) collective-permute-start(bf16[4,4,96,128]{3,2,1,0:T(8,128)(2,1)S(1)} %collective-permute-done.3), channel_id=1, source_target_pairs={{0,4},{1,5},{2,6},{3,7},{4,8},{5,9},{6,10},{7,11},{8,12},{9,13},{1... | collective-permute-start | bytes 1179656 | tf_op jit(solution)/shard_map/ppermute | solution.py:448
  32.8 10.4 %collective-permute-start.8 = (bf16[4,4,96,128]{3,2,1,0:T(8,128)(2,1)}, bf16[4,4,96,128]{3,2,1,0:T(8,128)(2,1)S(1)}, u32[]{:S(2)}, u32[]{:S(2)}) collective-permute-start(bf16[4,4,96,128]{3,2,1,0:T(8,128)(2,1)} %collective-permute-done.7), channel_id=1, source_target_pairs={{0,28},{1,29},{2,30},{3,31},{4,0},{5,1},{6,2},{7,3},{8,4},{9,5},{1... | collective-permute-start | bytes 1179656 | tf_op jit(solution)/shard_map/ppermute | solution.py:448
  36.4 10.2 %collective-permute-start.13 = (bf16[4,4,96,128]{3,2,1,0:T(8,128)(2,1)S(1)}, bf16[4,4,96,128]{3,2,1,0:T(8,128)(2,1)S(1)}, u32[]{:S(2)}, u32[]{:S(2)}) collective-permute-start(bf16[4,4,96,128]{3,2,1,0:T(8,128)(2,1)S(1)} %pad_maximum_fusion), channel_id=1, source_target_pairs={{0,128},{128,0},{1,129},{129,1},{2,130},{130,2},{3,131},{131,3},{4... | collective-permute-start | bytes 1179656 | tf_op jit(solution)/shard_map/ppermute | solution.py:452
  38.5 11.0 %collective-permute-start.19 = (bf16[4,4,96,128]{3,2,1,0:T(8,128)(2,1)S(1)}, bf16[4,4,96,128]{3,2,1,0:T(8,128)(2,1)S(1)}, u32[]{:S(2)}, u32[]{:S(2)}) collective-permute-start(bf16[4,4,96,128]{3,2,1,0:T(8,128)(2,1)S(1)} %collective-permute-done.3), channel_id=1, source_target_pairs={{0,128},{128,0},{1,129},{129,1},{2,130},{130,2},{3,131},{131,3},{4... | collective-permute-start | bytes 1179656 | tf_op jit(solution)/shard_map/ppermute | solution.py:452
  39.4 16.5 %collective-permute-start.20 = (bf16[4,4,96,128]{3,2,1,0:T(8,128)(2,1)}, bf16[4,4,96,128]{3,2,1,0:T(8,128)(2,1)S(1)}, u32[]{:S(2)}, u32[]{:S(2)}) collective-permute-start(bf16[4,4,96,128]{3,2,1,0:T(8,128)(2,1)} %collective-permute-done.7), channel_id=1, source_target_pairs={{0,128},{128,0},{1,129},{129,1},{2,130},{130,2},{3,131},{131,3},{4... | collective-permute-start | bytes 1179656 | tf_op jit(solution)/shard_map/ppermute | solution.py:452
  43.2 11.8 %collective-permute-start.5 = (bf16[4,4,96,128]{3,2,1,0:T(8,128)(2,1)S(1)}, bf16[4,4,96,128]{3,2,1,0:T(8,128)(2,1)S(1)}, u32[]{:S(2)}, u32[]{:S(2)}) collective-permute-start(bf16[4,4,96,128]{3,2,1,0:T(8,128)(2,1)S(1)} %collective-permute-done.4), channel_id=1, source_target_pairs={{0,4},{1,5},{2,6},{3,7},{4,8},{5,9},{6,10},{7,11},{8,12},{9,13},{1... | collective-permute-start | bytes 1179656 | tf_op jit(solution)/shard_map/ppermute | solution.py:448
  43.2 12.7 %collective-permute-start.9 = (bf16[4,4,96,128]{3,2,1,0:T(8,128)(2,1)S(1)}, bf16[4,4,96,128]{3,2,1,0:T(8,128)(2,1)S(1)}, u32[]{:S(2)}, u32[]{:S(2)}) collective-permute-start(bf16[4,4,96,128]{3,2,1,0:T(8,128)(2,1)S(1)} %collective-permute-done.8), channel_id=1, source_target_pairs={{0,28},{1,29},{2,30},{3,31},{4,0},{5,1},{6,2},{7,3},{8,4},{9,5},{1... | collective-permute-start | bytes 1179656 | tf_op jit(solution)/shard_map/ppermute | solution.py:448
  46.6 16.3 %collective-permute-start.17 = (bf16[4,4,96,128]{3,2,1,0:T(8,128)(2,1)S(1)}, bf16[4,4,96,128]{3,2,1,0:T(8,128)(2,1)S(1)}, u32[]{:S(2)}, u32[]{:S(2)}) collective-permute-start(bf16[4,4,96,128]{3,2,1,0:T(8,128)(2,1)S(1)} %collective-permute-done.4), channel_id=1, source_target_pairs={{0,128},{128,0},{1,129},{129,1},{2,130},{130,2},{3,131},{131,3},{4... | collective-permute-start | bytes 1179656 | tf_op jit(solution)/shard_map/ppermute | solution.py:452
  49.5 18.2 %collective-permute-start.18 = (bf16[4,4,96,128]{3,2,1,0:T(8,128)(2,1)S(1)}, bf16[4,4,96,128]{3,2,1,0:T(8,128)(2,1)S(1)}, u32[]{:S(2)}, u32[]{:S(2)}) collective-permute-start(bf16[4,4,96,128]{3,2,1,0:T(8,128)(2,1)S(1)} %collective-permute-done.8), channel_id=1, source_target_pairs={{0,128},{128,0},{1,129},{129,1},{2,130},{130,2},{3,131},{131,3},{4... | collective-permute-start | bytes 1179656 | tf_op jit(solution)/shard_map/ppermute | solution.py:452
  55.0 19.8 %collective-permute-start.15 = (bf16[4,4,96,128]{3,2,1,0:T(8,128)(2,1)S(1)}, bf16[4,4,96,128]{3,2,1,0:T(8,128)(2,1)S(1)}, u32[]{:S(2)}, u32[]{:S(2)}) collective-permute-start(bf16[4,4,96,128]{3,2,1,0:T(8,128)(2,1)S(1)} %collective-permute-done.5), channel_id=1, source_target_pairs={{0,128},{128,0},{1,129},{129,1},{2,130},{130,2},{3,131},{131,3},{4... | collective-permute-start | bytes 1179656 | tf_op jit(solution)/shard_map/ppermute | solution.py:452
  55.9 18.9 %collective-permute-start.16 = (bf16[4,4,96,128]{3,2,1,0:T(8,128)(2,1)S(1)}, bf16[4,4,96,128]{3,2,1,0:T(8,128)(2,1)S(1)}, u32[]{:S(2)}, u32[]{:S(2)}) collective-permute-start(bf16[4,4,96,128]{3,2,1,0:T(8,128)(2,1)S(1)} %collective-permute-done.9), channel_id=1, source_target_pairs={{0,128},{128,0},{1,129},{129,1},{2,130},{130,2},{3,131},{131,3},{4... | collective-permute-start | bytes 1179656 | tf_op jit(solution)/shard_map/ppermute | solution.py:452
  62.7 11.5 %collective-permute-start.6 = (bf16[2,4,96,128]{3,2,1,0:T(8,128)(2,1)S(1)}, bf16[2,4,96,128]{3,2,1,0:T(8,128)(2,1)S(1)}, u32[]{:S(2)}, u32[]{:S(2)}) collective-permute-start(bf16[2,4,96,128]{3,2,1,0:T(8,128)(2,1)S(1)} %slice.8), channel_id=1, source_target_pairs={{0,4},{1,5},{2,6},{3,7},{4,8},{5,9},{6,10},{7,11},{8,12},{9,13},{1... | collective-permute-start | bytes 589832 | tf_op jit(solution)/shard_map/ppermute | solution.py:448
  62.9 11.5 %collective-permute-start.10 = (bf16[2,4,96,128]{3,2,1,0:T(8,128)(2,1)S(1)}, bf16[2,4,96,128]{3,2,1,0:T(8,128)(2,1)S(1)}, u32[]{:S(2)}, u32[]{:S(2)}) collective-permute-start(bf16[2,4,96,128]{3,2,1,0:T(8,128)(2,1)S(1)} %slice.9), channel_id=1, source_target_pairs={{0,28},{1,29},{2,30},{3,31},{4,0},{5,1},{6,2},{7,3},{8,4},{9,5},{1... | collective-permute-start | bytes 589832 | tf_op jit(solution)/shard_map/ppermute | solution.py:448
  74.2 7.9 %collective-permute-start.11 = (bf16[2,4,96,128]{3,2,1,0:T(8,128)(2,1)S(1)}, bf16[2,4,96,128]{3,2,1,0:T(8,128)(2,1)S(1)}, u32[]{:S(2)}, u32[]{:S(2)}) collective-permute-start(bf16[2,4,96,128]{3,2,1,0:T(8,128)(2,1)S(1)} %collective-permute-done.6), channel_id=1, source_target_pairs={{0,128},{128,0},{1,129},{129,1},{2,130},{130,2},{3,131},{131,3},{4... | collective-permute-start | bytes 589832 | tf_op jit(solution)/shard_map/ppermute | solution.py:452
  74.3 7.8 %collective-permute-start.12 = (bf16[2,4,96,128]{3,2,1,0:T(8,128)(2,1)S(1)}, bf16[2,4,96,128]{3,2,1,0:T(8,128)(2,1)S(1)}, u32[]{:S(2)}, u32[]{:S(2)}) collective-permute-start(bf16[2,4,96,128]{3,2,1,0:T(8,128)(2,1)S(1)} %collective-permute-done.10), channel_id=1, source_target_pairs={{0,128},{128,0},{1,129},{129,1},{2,130},{130,2},{3,131},{131,3},{4... | collective-permute-start | bytes 589832 | tf_op jit(solution)/shard_map/ppermute | solution.py:452
  (7 other events, 113.5 us)
